TPU v7x, 32 devices: a whole 2x2x4 slice. The times are simulated.
32 devices in a mesh: tm: 8 (over y, x, core), diag: 4 (over z).
Axes of the slice: x: 2, y: 2, z: 4, core: 2. Of those that a mesh axis runs over, the one named last changes fastest.
Arguments:
- series: float32 [131072], P('tm'), may hold values from -6 to 6
- tail: float32 [256], replicated, may hold values from -6 to 6
- diag_offsets: int32 [4], P('diag'), may hold values from 0 to 12000, as said below
- exclusion: int32 [1], replicated, may hold values from 64 to 255
Outputs:
- profile: float32 [131072], P(('tm', 'diag'))
Inputs may be any that keep to these rules, and one draw needn't show every extreme that they name: `diag_offsets`: in every draw some group starts at 12000 and another below 64; the others anywhere in the range, blocks may intersect.
All inputs are finite; a program needn't handle non-finite values.
Results may differ from a plain program's by a relative error of at most 0.0003.
Values sent between devices are 32-bit elements; how exact they have to be, the bound alone decides.
No kernel may reach another device: no remote copies, remote signals or barrier semaphores. Data moves between devices by JAX's collectives and lax.ppermute only.
A program may use at most 64 MiB of HBM per device.

v0:
```python
import jax
import jax.numpy as jnp
from jax import lax
from jax.sharding import PartitionSpec as P

M = 256
KB = 32
RB = 8192


FILL = 1e30


def passed_along(shard, axis, by):
    size = lax.axis_size(axis)
    pairs = [(i, i + by) for i in range(size) if 0 <= i + by < size]
    return lax.ppermute(shard, axis, pairs)


def window_stats(extended):
    count = extended.shape[0] // M
    blocks = jnp.concatenate([extended, jnp.zeros((M,), jnp.float32)]).reshape(count + 1, M)
    row_ids = lax.broadcasted_iota(jnp.int32, (M, M), 0)
    col_ids = lax.broadcasted_iota(jnp.int32, (M, M), 1)
    upper = (row_ids >= col_ids).astype(jnp.float32)
    lower = (row_ids < col_ids).astype(jnp.float32)

    def window_sums(values):
        head = jnp.dot(
            values[:-1], upper, precision=lax.Precision.HIGHEST, preferred_element_type=jnp.float32
        )
        after = jnp.dot(
            values[1:], lower, precision=lax.Precision.HIGHEST, preferred_element_type=jnp.float32
        )
        return (head + after).reshape(-1)

    first = window_sums(blocks) / M
    second = window_sums(blocks * blocks) / M
    return (first, 1.0 / jnp.sqrt(second - first * first + 1e-05))


def hankel(vector, height, width):
    span = height + width
    tiled = jnp.tile(vector, height + 1)[: height * (span + 1)]
    return tiled.reshape(height, span + 1)[:, :width]


def skew(matrix):
    height, width = matrix.shape
    padded = jnp.concatenate([matrix, jnp.full((height, height), FILL, matrix.dtype)], axis=1)
    flat = padded.reshape(-1)[: height * (width + height - 1)]
    return flat.reshape(height, width + height - 1)


def running_sums(values):
    height, width = values.shape
    inner = 128
    grouped = values.reshape(height, width // inner, inner)
    within = jnp.cumsum(grouped, axis=2) - grouped
    totals = jnp.sum(grouped, axis=2)
    before = jnp.cumsum(totals, axis=1) - totals
    return ((within + before[:, :, None]).reshape(height, width), jnp.sum(totals, axis=1))


def block_terms(extended, offset, row_start, rows):
    leading = lax.dynamic_slice_in_dim(extended, row_start, rows + M)
    partner = hankel(
        lax.dynamic_slice_in_dim(extended, row_start + offset, KB + rows + M), KB, rows + M
    )
    return leading[None, M:] * partner[:, M:] - leading[None, :rows] * partner[:, :rows]


def first_products(extended, offset):
    partner = hankel(lax.dynamic_slice_in_dim(extended, offset, KB + M), KB, M)
    return jnp.dot(
        partner, extended[:M], precision=lax.Precision.HIGHEST, preferred_element_type=jnp.float32
    )


def sweep(extended, means, spreads, offset, exclusion_width, limit, start, segment):
    rows = min(RB, segment)
    diag_ids = lax.broadcasted_iota(jnp.int32, (KB, rows), 0)
    row_ids = lax.broadcasted_iota(jnp.int32, (KB, rows), 1)

    def advance(index, carry):
        current, row_best, column_best = carry
        row_start = (index * rows).astype(jnp.int32)
        change = block_terms(extended, offset, row_start, rows)
        running, total = running_sums(change)
        products = current[:, None] + running
        mean_row = lax.dynamic_slice_in_dim(means, row_start, rows)
        spread_row = lax.dynamic_slice_in_dim(spreads, row_start, rows)
        mean_pair = hankel(lax.dynamic_slice_in_dim(means, row_start + offset, KB + rows), KB, rows)
        spread_pair = hankel(
            lax.dynamic_slice_in_dim(spreads, row_start + offset, KB + rows), KB, rows
        )
        corr = (products / M - mean_row[None, :] * mean_pair) * (spread_row[None, :] * spread_pair)
        distance = jnp.sqrt(1.0 - corr)
        partner_pos = row_start + offset + diag_ids + row_ids
        counted = (offset + diag_ids >= exclusion_width) & (partner_pos < limit)
        masked = jnp.where(counted, distance, FILL)
        row_best = lax.dynamic_update_slice_in_dim(row_best, jnp.min(masked, axis=0), row_start, 0)
        column_block = jnp.min(skew(masked), axis=0)
        column_start = row_start + offset
        previous = lax.dynamic_slice_in_dim(column_best, column_start, rows + KB - 1)
        column_best = lax.dynamic_update_slice_in_dim(
            column_best, jnp.minimum(previous, column_block), column_start, 0
        )
        return (current + total, row_best, column_best)

    initial = (
        start,
        jnp.full((segment,), FILL, jnp.float32),
        jnp.full((extended.shape[0],), FILL, jnp.float32),
    )
    result = lax.fori_loop(0, segment // rows, advance, initial)
    return (result[1], result[2])


def on_device(series, tail, diag_offsets, exclusion):
    segment = series.shape[0]
    reach = segment // 2 + segment // 4
    position = lax.axis_index("tm")
    final_place = lax.axis_size("tm") - 1
    ahead = passed_along(series[:reach], "tm", -1)
    tail_block = jnp.concatenate([tail, jnp.zeros((reach - tail.shape[0],), jnp.float32)])
    ahead = jnp.where(position == final_place, tail_block, ahead)
    extended = jnp.concatenate([series, ahead])
    means, spreads = window_stats(extended)
    offset = diag_offsets[0]
    exclusion_width = exclusion[0]
    limit = jnp.where(position == final_place, segment, segment + reach).astype(jnp.int32)
    start = first_products(extended, offset)
    row_best, column_best = sweep(
        extended, means, spreads, offset, exclusion_width, limit, start, segment
    )
    spilled = passed_along(column_best[segment:], "tm", 1)
    spilled = jnp.where(position == 0, FILL, spilled)
    spilled = jnp.concatenate([spilled, jnp.full((segment - reach,), FILL, jnp.float32)])
    owned = jnp.minimum(jnp.minimum(row_best, column_best[:segment]), spilled)
    groups = lax.axis_size("diag")
    share = segment // groups
    received = lax.all_to_all(owned, "diag", split_axis=0, concat_axis=0, tiled=True)
    return jnp.min(received.reshape(groups, share), axis=0)


def solution(mesh):
    in_specs = (P("tm"), P(), P("diag"), P())
    out_specs = P(("tm", "diag"))
    return jax.shard_map(
        on_device, mesh=mesh, in_specs=in_specs, out_specs=out_specs, check_vma=False
    )
```

profile of v0, /device:TPU:4, one launch (start us, length us, event | category | flops | bytes accessed | tf_op | source)
XLA Modules:
  0.0 98.2 jit_solution(7543158521432953929)
XLA Ops:
  0.0 0.9 slice.126
  0.9 2.8 %collective-permute-start = (f32[12288]{0:T(1024)S(1)}, f32[12288]{0:T(1024)S(1)}, u32[]{:S(2)}, u32[]{:S(2)}) collective-permute-start(f32[12288]{0:T(1024)S(1)} %slice.126), channel_id=1, source_target_pairs={{4,0},{8,4},{12,8},{16,12},{20,16},{24,20},{28,24},{5,1},{9,5},{13... | collective-permute-start | bytes 147464 | tf_op jit(solution)/shard_map/ppermute | solution.py:17
  4.3 1.1 %collective-permute-done = f32[12288]{0:T(1024)S(1)} collective-permute-done((f32[12288]{0:T(1024)S(1)}, f32[12288]{0:T(1024)S(1)}, u32[]{:S(2)}, u32[]{:S(2)}) %collective-permute-start) | collective-permute-done | bytes 49184 | tf_op jit(solution)/shard_map/ppermute | solution.py:17
  5.4 0.7 pad_select_fusion
  6.1 0.8 pad_maximum_fusion
  6.9 0.8 fusion.23
  9.3 0.7 convolution_bitcast_fusion
  11.3 67.8 %while.19 = (s32[]{:T(128)}, f32[32]{0:T(128)}, f32[16384]{0:T(1024)}, f32[28672]{0:T(1024)}, f32[28672]{0:T(1024)S(1)}, /*index=5*/s32[]{:T(128)}, s32[]{:T(128...) while((s32[]{:T(128)}, f32[32]{0:T(128)}, ...), condition=%wide.region_7.8_spmd.clone.clone, body=%wide.region_0.7_spmd.clone.clone.sunk | while | flops 39443432 | bytes 52372300 | solution.py:116
  13.0 1.7 %reshape.124 = f32[32,8225]{1,0:T(8,128)} reshape(f32[263200]{0:T(1024)S(1)} %slice.198) | data formatting | bytes 2105600 | tf_op jit(solution)/shard_map/while/body/eval_jaxpr/reshape | solution.py:45
  15.3 1.7 %reshape.123 = f32[32,8225]{1,0:T(8,128)} reshape(f32[263200]{0:T(1024)S(1)} %slice.197) | data formatting | bytes 2105600 | tf_op jit(solution)/shard_map/while/body/eval_jaxpr/reshape | solution.py:45
  17.1 0.8 tile.99
  18.0 0.7 reshape.122
  18.7 0.8 fusion.40
  20.1 14.7 %reduce_window_sum.39 = f32[32,64,128]{2,1,0:T(8,128)} reduce-window(f32[32,64,128]{2,1,0:T(8,128)S(1)} %bitcast.59, f32[]{:T(128)} %constant.96.clone.1..sunk), window={size=1x1x128 pad=0_0x0_0x127_0}, to_apply=%region_2.2 | reduce-window | flops 33292288 | bytes 2097156 | tf_op jit(solution)/shard_map/while/body/eval_jaxpr/jit(cumsum)/reduce_window_sum | solution.py:59
  36.0 5.0 %fusion.41 = (f32[8192]{0:T(1024)S(1)}, f32[32,8192]{1,0:T(8,128)S(1)}) fusion(f32[32,8225]{1,0:T(8,128)} %reshape.123, f32[8192]{0:T(1024)S(1)} %dynamic_slice.85, f32[32,8225]{1,0:T(8,128)S(1)} %copy-done, f32[8192]{0:T(1024)S(1)} %dynamic_slice.87, f32[4,8,64,128]{3,2,1,0:T(8,128)S(1)} %bitcast.63, f32[32,8192]{1,0:T(8,128)S(1)} %get-tuple-element.361, ...), kind=kLoop, calls=%fused_computation.45.clone.1 | loop fusion | flops 4448256 | bytes 6389904 | tf_op jit(solution)/shard_map/while/body/eval_jaxpr/reduce_min | solution.py:102
  42.8 0.7 reshape.126
  43.6 1.6 %minimum_dynamic-update-slice_fusion.2 = f32[28672]{0:T(1024)} fusion(f32[28672]{0:T(1024)} %get-tuple-element.386, s32[]{:T(128)S(6)} %select_n.81, f32[8223]{0:T(1024)S(1)} %reduce_min.44), kind=kLoop, calls=%fused_computation.22.clone.1 | loop fusion | flops 8223 | bytes 106624 | tf_op jit(solution)/shard_map/while/body/eval_jaxpr/dynamic_update_slice | solution.py:106
  46.9 1.7 %reshape.124 = f32[32,8225]{1,0:T(8,128)} reshape(f32[263200]{0:T(1024)S(1)} %slice.198) | data formatting | bytes 2105600 | tf_op jit(solution)/shard_map/while/body/eval_jaxpr/reshape | solution.py:45
  49.3 1.7 %reshape.123 = f32[32,8225]{1,0:T(8,128)} reshape(f32[263200]{0:T(1024)S(1)} %slice.197) | data formatting | bytes 2105600 | tf_op jit(solution)/shard_map/while/body/eval_jaxpr/reshape | solution.py:45
  51.0 0.8 tile.99
  52.0 0.7 reshape.122
  52.7 0.8 fusion.40
  54.0 14.7 %reduce_window_sum.39 = f32[32,64,128]{2,1,0:T(8,128)} reduce-window(f32[32,64,128]{2,1,0:T(8,128)S(1)} %bitcast.59, f32[]{:T(128)} %constant.96.clone.1..sunk), window={size=1x1x128 pad=0_0x0_0x127_0}, to_apply=%region_2.2 | reduce-window | flops 33292288 | bytes 2097156 | tf_op jit(solution)/shard_map/while/body/eval_jaxpr/jit(cumsum)/reduce_window_sum | solution.py:59
  70.0 5.0 %fusion.41 = (f32[8192]{0:T(1024)S(1)}, f32[32,8192]{1,0:T(8,128)S(1)}) fusion(f32[32,8225]{1,0:T(8,128)} %reshape.123, f32[8192]{0:T(1024)S(1)} %dynamic_slice.85, f32[32,8225]{1,0:T(8,128)S(1)} %copy-done, f32[8192]{0:T(1024)S(1)} %dynamic_slice.87, f32[4,8,64,128]{3,2,1,0:T(8,128)S(1)} %bitcast.63, f32[32,8192]{1,0:T(8,128)S(1)} %get-tuple-element.361, ...), kind=kLoop, calls=%fused_computation.45.clone.1 | loop fusion | flops 4448256 | bytes 6389904 | tf_op jit(solution)/shard_map/while/body/eval_jaxpr/reduce_min | solution.py:102
  76.7 0.7 reshape.126
  77.5 1.6 %minimum_dynamic-update-slice_fusion.2 = f32[28672]{0:T(1024)} fusion(f32[28672]{0:T(1024)} %get-tuple-element.386, s32[]{:T(128)S(6)} %select_n.81, f32[8223]{0:T(1024)S(1)} %reduce_min.44), kind=kLoop, calls=%fused_computation.22.clone.1 | loop fusion | flops 8223 | bytes 106624 | tf_op jit(solution)/shard_map/while/body/eval_jaxpr/dynamic_update_slice | solution.py:106
  79.1 0.8 slice.138
  79.9 2.7 %collective-permute-start.1 = (f32[12288]{0:T(1024)S(1)}, f32[12288]{0:T(1024)S(1)}, u32[]{:S(2)}, u32[]{:S(2)}) collective-permute-start(f32[12288]{0:T(1024)S(1)} %slice.138), channel_id=1, source_target_pairs={{0,4},{4,8},{8,12},{12,16},{16,20},{20,24},{24,28},{1,5},{5,9},{9,... | collective-permute-start | bytes 147464 | tf_op jit(solution)/shard_map/ppermute | solution.py:17
  82.6 3.7 %collective-permute-done.1 = f32[12288]{0:T(1024)S(1)} collective-permute-done((f32[12288]{0:T(1024)S(1)}, f32[12288]{0:T(1024)S(1)}, u32[]{:S(2)}, u32[]{:S(2)}) %collective-permute-start.1) | collective-permute-done | bytes 49184 | tf_op jit(solution)/shard_map/ppermute | solution.py:17
  86.3 0.9 pad_minimum_fusion
  87.1 10.4 %all_to_all.9 = f32[4,4096,1]{1,2,0:T(1,128)S(1)} all-to-all(f32[4,4096,1]{1,2,0:T(1,128)S(1)} %bitcast.68), channel_id=1, replica_groups=mesh['tm'=8,'diag'=4] {'diag'}, dimensions={0} | all-to-all | bytes 131072 | tf_op jit(solution)/shard_map/all_to_all | solution.py:143
  97.5 0.7 reduce_min.35
  (105 shorter events, 13.2 us)
Async XLA Ops:
  0.0 8.0 %copy-start.3 = (f32[16384]{0:T(1024)S(1)}, f32[16384]{0:T(1024)}, u32[]{:S(2)}) copy-start(f32[16384]{0:T(1024)} %param.6) | copy-start | bytes 196612
  0.9 4.5 %collective-permute-start = (f32[12288]{0:T(1024)S(1)}, f32[12288]{0:T(1024)S(1)}, u32[]{:S(2)}, u32[]{:S(2)}) collective-permute-start(f32[12288]{0:T(1024)S(1)} %slice.126), channel_id=1, source_target_pairs={{4,0},{8,4},{12,8},{16,12},{20,16},{24,20},{28,24},{5,1},{9,5},{13... | collective-permute-start | bytes 147464 | tf_op jit(solution)/shard_map/ppermute | solution.py:17
  8.1 1.2 %slice-start = ((f32[16384]{0:T(1024)}), f32[256]{0:T(256)S(1)}, s32[]{:S(2)}) async-start(f32[16384]{0:T(1024)} %param.6), calls=%async_computation.1 | async-start | bytes 2048 | tf_op jit(solution)/shard_map/slice | solution.py:76
  11.3 0.7 copy-start.1
  34.8 1.2 %copy-start = (f32[32,8225]{1,0:T(8,128)S(1)}, f32[32,8225]{1,0:T(8,128)}, u32[]{:S(2)}) copy-start(f32[32,8225]{1,0:T(8,128)} %reshape.124) | copy-start | bytes 3158404 | tf_op jit(solution)/shard_map/while
  34.8 1.2 %copy-start.6 = (f32[32]{0:T(128)S(1)}, f32[32]{0:T(128)}, u32[]{:S(2)}) copy-start(f32[32]{0:T(128)} %get-tuple-element.384) | copy-start | bytes 388 | tf_op jit(solution)/shard_map/while
  36.0 5.1 %copy-start.8 = (f32[32]{0:T(128)S(1)}, f32[32]{0:T(128)}, u32[]{:S(2)}) copy-start(f32[32]{0:T(128)} %get-tuple-element.360) | copy-start | bytes 388 | tf_op jit(solution)/shard_map/while
  36.0 5.7 %copy-start.4 = (f32[16384]{0:T(1024)S(1)}, f32[16384]{0:T(1024)}, u32[]{:S(2)}) copy-start(f32[16384]{0:T(1024)} %get-tuple-element.385) | copy-start | bytes 196612 | tf_op jit(solution)/shard_map/while
  41.1 0.6 copy-start.7
  42.2 0.6 copy-start.5
  43.5 1.8 %copy-start.2 = (f32[28672]{0:T(1024)S(1)}, f32[28672]{0:T(1024)}, u32[]{:S(2)}) copy-start(f32[28672]{0:T(1024)} %copy-done.1) | copy-start | bytes 344068 | tf_op jit(solution)/shard_map/while
  45.3 0.7 copy-start.1
  68.8 1.2 %copy-start = (f32[32,8225]{1,0:T(8,128)S(1)}, f32[32,8225]{1,0:T(8,128)}, u32[]{:S(2)}) copy-start(f32[32,8225]{1,0:T(8,128)} %reshape.124) | copy-start | bytes 3158404 | tf_op jit(solution)/shard_map/while
  68.8 1.2 %copy-start.6 = (f32[32]{0:T(128)S(1)}, f32[32]{0:T(128)}, u32[]{:S(2)}) copy-start(f32[32]{0:T(128)} %get-tuple-element.384) | copy-start | bytes 388 | tf_op jit(solution)/shard_map/while
  70.0 5.1 %copy-start.8 = (f32[32]{0:T(128)S(1)}, f32[32]{0:T(128)}, u32[]{:S(2)}) copy-start(f32[32]{0:T(128)} %get-tuple-element.360) | copy-start | bytes 388 | tf_op jit(solution)/shard_map/while
  70.0 5.7 %copy-start.4 = (f32[16384]{0:T(1024)S(1)}, f32[16384]{0:T(1024)}, u32[]{:S(2)}) copy-start(f32[16384]{0:T(1024)} %get-tuple-element.385) | copy-start | bytes 196612 | tf_op jit(solution)/shard_map/while
  75.1 0.6 copy-start.7
  76.1 0.6 copy-start.5
  77.4 1.8 %copy-start.2 = (f32[28672]{0:T(1024)S(1)}, f32[28672]{0:T(1024)}, u32[]{:S(2)}) copy-start(f32[28672]{0:T(1024)} %copy-done.1) | copy-start | bytes 344068 | tf_op jit(solution)/shard_map/while
  79.9 6.3 %collective-permute-start.1 = (f32[12288]{0:T(1024)S(1)}, f32[12288]{0:T(1024)S(1)}, u32[]{:S(2)}, u32[]{:S(2)}) collective-permute-start(f32[12288]{0:T(1024)S(1)} %slice.138), channel_id=1, source_target_pairs={{0,4},{4,8},{8,12},{12,16},{16,20},{20,24},{24,28},{1,5},{5,9},{9,... | collective-permute-start | bytes 147464 | tf_op jit(solution)/shard_map/ppermute | solution.py:17
where the time goes:
time: 99 us; the launch traced here: 98.2 us
  other arithmetic  49.7 us (50%)
  local copies, waits for them, and re-layouts  23.7 us (24%)
  blocking collectives  10.4 us (11%)
  starting transfers between devices  5.43 us (5%)
  waiting for transfers between devices  4.73 us (5%)
  loops' own time  1.69 us (2%)
  matrix products  1.64 us (2%)
    another operation x2, other arithmetic, running_sums(): within = jnp.cumsum(grouped, axis=2) - grouped  29.4 us
    all_to_all x1, blocking collectives, on_device(): lax.all_to_all(owned, 'diag', split_axis=0, concat_axis=0, tiled=True)  10.4 us
    reduce_min x2, other arithmetic, advance(): jnp.min(masked, axis=0)  10.1 us
    reshape x7, local copies, waits for them, and re-layouts, hankel(): return tiled.reshape(height, span + 1)[:, :width]  8.32 us
    ppermute x2, starting transfers between devices, passed_along(): return lax.ppermute(shard, axis, pairs)  5.43 us
    ppermute x2, waiting for transfers between devices, passed_along(): return lax.ppermute(shard, axis, pairs)  4.73 us
    another operation x14, local copies, waits for them, and re-layouts, hankel(): tiled = jnp.tile(vector, height + 1)[:height * (span + 1)]  4.04 us
    dynamic_update_slice x2, other arithmetic, advance(): lax.dynamic_update_slice_in_dim(column_best, jnp.minimum(previous, column...  3.27 us
  transfers between devices with their start and end apart: 2, of which 2 were waited for; matrix products, arithmetic and copies ran while one was open for 0% of the time, Pallas kernels for 0%

commit v1 on v0

v1 whole, which is shorter than its diff:
```python
import functools

import jax
import jax.numpy as jnp
from jax import lax
from jax.experimental import pallas as pl
from jax.experimental.pallas import tpu as pltpu
from jax.sharding import PartitionSpec as P

M = 256
KB = 32
FILL = 1e30
LANES = 128
SUB = 8
STEP = KB // SUB
WROWS = LANES + KB
XROWS = LANES + KB + M
BIG = 1e30
UNROLL = 8


def shifted(shard, axis, by):
    size = lax.axis_size(axis)
    return lax.ppermute(shard, axis, [(i, (i + by) % size) for i in range(size)])


def swapped(shard, axis, bit):
    size = lax.axis_size(axis)
    return lax.ppermute(shard, axis, [(i, i ^ bit) for i in range(size)])


def group_offsets(own):
    size = lax.axis_size("diag")
    slots = jnp.where(lax.iota(jnp.int32, LANES) == lax.axis_index("diag"), own[0], 0)
    bit = 1
    while bit < size:
        slots = slots + swapped(slots, "diag", bit)
        bit *= 2
    return slots


def split3(x):
    hi = x.astype(jnp.bfloat16)
    rest = x - hi.astype(jnp.float32)
    mid = rest.astype(jnp.bfloat16)
    low = (rest - mid.astype(jnp.float32)).astype(jnp.bfloat16)
    return hi, mid, low


def window_pieces(x, ones):
    out = None
    for piece in split3(x):
        part = jnp.dot(piece, ones, preferred_element_type=jnp.float32)
        out = part if out is None else out + part
    return out


def kernel(geo, offs_ref, excl_ref, left_ref, own_ref, right_ref, tail_ref, out_ref,
           ext, sums, text, stext, utext, xband, sband, uband, pband, xown, mown, best):
    segrows, share_rows, back, nrows, groups, places = geo
    place = lax.axis_index("tm")
    diag = lax.axis_index("diag")
    excl = excl_ref[0]

    ext[0:segrows, :] = left_ref[...]
    ext[segrows : 2 * segrows, :] = own_ref[...]
    last = place == places - 1

    @pl.when(last)
    def _():
        tail_rows = M // LANES
        ext[2 * segrows : 2 * segrows + tail_rows, :] = tail_ref[...]
        ext[2 * segrows + tail_rows : 3 * segrows, :] = jnp.zeros(
            (segrows - tail_rows, LANES), jnp.float32
        )

    @pl.when(jnp.logical_not(last))
    def _():
        ext[2 * segrows : 3 * segrows, :] = right_ref[...]

    if ext.shape[0] > 3 * segrows:
        ext[3 * segrows :, :] = jnp.zeros((ext.shape[0] - 3 * segrows, LANES), jnp.float32)
    first_row = pl.multiple_of(segrows - back + share_rows * diag, SUB)
    x = ext[pl.ds(first_row, 2 * LANES), :]

    rid = lax.broadcasted_iota(jnp.int32, (LANES, 2 * LANES), 0)
    cid = lax.broadcasted_iota(jnp.int32, (LANES, 2 * LANES), 1)
    ones = jnp.where(
        cid < LANES, (rid >= cid).astype(jnp.float32), (rid < cid - LANES).astype(jnp.float32)
    ).astype(jnp.bfloat16)
    held = 2 * LANES - SUB

    def windows(values):
        sums[...] = window_pieces(values, ones)
        return (
            sums[0:held, 0:LANES]
            + (sums[1 : held + 1, 0:LANES] + sums[1 : held + 1, LANES:])
            + sums[2 : held + 2, LANES:]
        )

    mean = windows(x) * (1.0 / M)
    second = windows(x * x) * (1.0 / M)
    spread = lax.rsqrt(second - mean * mean + 1e-05)
    pad = jnp.zeros((SUB, LANES), jnp.float32)

    def turned(values):
        return jnp.concatenate([values[0:LANES].T, values[LANES:].T], axis=1)

    xt = turned(x)
    mt = turned(jnp.concatenate([mean, pad], axis=0))
    st = turned(jnp.concatenate([spread, pad], axis=0))
    ut = mt * st
    st256 = st * (1.0 / M)

    def spread_out(ref, values, turns):
        for tile in range(3):
            for n in range(turns):
                by = (LANES // 2) * tile + n
                moved = pltpu.roll(values, (2 * LANES - by) % (2 * LANES), 1) if by else values
                ref[tile, n * LANES : (n + 1) * LANES, :] = moved[:, 0:LANES]

    spread_out(text, xt, 5)
    spread_out(stext, st256, 3)
    spread_out(utext, ut, 3)

    lane = lax.broadcasted_iota(jnp.int32, (LANES, LANES), 1)

    def own_rows(values, n):
        moved = pltpu.roll(values, (2 * LANES - back - n) % (2 * LANES), 1)[:, 0:LANES]
        width = share_rows
        while width < LANES:
            moved = jnp.where((lane & width) != 0, pltpu.roll(moved, width, 1), moved)
            width *= 2
        return moved

    for n in range(3):
        xown[n * LANES : (n + 1) * LANES, :] = own_rows(xt, n)
    mown[...] = own_rows(mt, 0)
    spread_own = own_rows(st, 0)

    lane8 = lax.broadcasted_iota(jnp.int32, (1, LANES), 1)
    sub8 = lax.broadcasted_iota(jnp.int32, (SUB, LANES), 0)
    limit = places * segrows * LANES
    own_start = (place * segrows + share_rows * diag) * LANES
    lane_row = (lane8 & (share_rows - 1)) * LANES
    hide = []
    for way in range(2):
        first_lag = jnp.zeros((1, LANES), jnp.int32)
        lo = jnp.zeros((1, LANES), jnp.int32)
        xs = ss = us = None
        for g in range(groups):
            off = offs_ref[g]
            lag = off if way == 0 else -(off + (KB - 1))
            base = back * LANES + lag
            col = base // LANES
            row = base - col * LANES
            tile = col // (LANES // 2)
            turn = (share_rows * g - (col - tile * (LANES // 2)) + LANES) % LANES
            here = (lane8 >= share_rows * g) & (lane8 < share_rows * (g + 1))
            first_lag = jnp.where(here, lag, first_lag)

            def merged(ref, rows, acc):
                part = pltpu.roll(ref[tile, pl.ds(row, rows), :], turn, 1)
                return part if acc is None else jnp.where(here, part, acc)

            xs = merged(text, XROWS, xs)
            ss = merged(stext, WROWS, ss)
            us = merged(utext, WROWS, us)
        xband[way] = xs
        sband[way] = ss
        uband[way] = us
        position = (
            own_start + lane_row + first_lag + lax.broadcasted_iota(jnp.int32, (WROWS, LANES), 0)
        )
        pband[way] = jnp.where((position >= 0) & (position < limit), BIG, -BIG)
        for s in range(STEP):
            lag = first_lag + STEP * sub8 + s
            hide.append(jnp.abs(lag) < excl)

    chains = 2 * STEP

    def band(ref, way, start):
        return ref[way, pl.ds(start, SUB, stride=STEP), :]

    def row(ref, i):
        return ref[pl.ds(i, SUB, stride=0), :]

    def first(step, sums_):
        sums_ = list(sums_)
        for u in range(UNROLL):
            i = step * UNROLL + u
            xi = row(xown, i)
            for way in range(2):
                for s in range(STEP):
                    c = way * STEP + s
                    sums_[c] = sums_[c] + xi * band(xband, way, i + s)
        return tuple(sums_)

    zero = jnp.zeros((SUB, LANES), jnp.float32)
    start = lax.fori_loop(0, M // UNROLL, first, (zero,) * chains)
    start = tuple(jnp.where(h, -BIG, q) for h, q in zip(hide, start))

    def advance(step, products):
        products = list(products)
        for u in range(UNROLL):
            i = step * UNROLL + u
            xi = row(xown, i)
            xn = row(xown, i + M)
            mi = row(mown, i)
            top = None
            for way in range(2):
                for s in range(STEP):
                    c = way * STEP + s
                    q = products[c]
                    value = q * band(sband, way, i + s) - mi * band(uband, way, i + s)
                    value = jnp.minimum(value, band(pband, way, i + s))
                    top = value if top is None else jnp.maximum(top, value)
                    products[c] = q + (
                        xn * band(xband, way, i + s + M) - xi * band(xband, way, i + s)
                    )
            best[pl.ds(pl.multiple_of(i * SUB, SUB), SUB), :] = top
        return tuple(products)

    lax.fori_loop(0, LANES // UNROLL, advance, start)

    blocks = []
    for block in range(LANES // SUB):
        top = None
        for h in range(SUB):
            part = best[pl.ds(block * SUB * SUB + h, SUB, stride=SUB), :]
            top = part if top is None else jnp.maximum(top, part)
        blocks.append(top)
    top = jnp.concatenate(blocks, axis=0)
    width = share_rows
    while width < LANES:
        top = jnp.maximum(top, pltpu.roll(top, width, 1))
        width *= 2
    distance = jnp.sqrt(jnp.maximum(1.0 - top * spread_own, 0.0))
    distance = jnp.where(top < -1e20, FILL, distance)
    out_ref[...] = distance.T[0:share_rows, :]


def on_device(series, tail, diag_offsets, exclusion):
    segment = series.shape[0]
    groups = lax.axis_size("diag")
    places = lax.axis_size("tm")
    reach = segment // 2 + segment // 4
    segrows = segment // LANES
    share_rows = segrows // groups
    back = reach // LANES
    deepest = segrows - back + share_rows * (groups - 1)
    geo = (segrows, share_rows, back, 2 * back + share_rows, groups, places)
    left = shifted(series, "tm", 1)
    right = shifted(series, "tm", -1)
    offsets = group_offsets(diag_offsets)
    f32 = jnp.float32
    rows = lambda a: a.reshape(-1, LANES)
    smem = pl.BlockSpec(memory_space=pltpu.SMEM)
    vmem = pl.BlockSpec(memory_space=pltpu.VMEM)
    out = pl.pallas_call(
        functools.partial(kernel, geo),
        out_shape=jax.ShapeDtypeStruct((share_rows, LANES), f32),
        in_specs=[smem, smem, vmem, vmem, vmem, vmem],
        out_specs=vmem,
        scratch_shapes=[
            pltpu.VMEM((max(3 * segrows, deepest + 2 * LANES), LANES), f32),
            pltpu.VMEM((2 * LANES, 2 * LANES), f32),
            pltpu.VMEM((3, 5 * LANES, LANES), f32),
            pltpu.VMEM((3, 3 * LANES, LANES), f32),
            pltpu.VMEM((3, 3 * LANES, LANES), f32),
            pltpu.VMEM((2, XROWS, LANES), f32),
            pltpu.VMEM((2, WROWS, LANES), f32),
            pltpu.VMEM((2, WROWS, LANES), f32),
            pltpu.VMEM((2, WROWS, LANES), f32),
            pltpu.VMEM((3 * LANES, LANES), f32),
            pltpu.VMEM((LANES, LANES), f32),
            pltpu.VMEM((LANES * SUB, LANES), f32),
        ],
    )(offsets, exclusion, rows(left), rows(series), rows(right), rows(tail))
    return out.reshape(-1)


def solution(mesh):
    in_specs = (P("tm"), P(), P("diag"), P())
    out_specs = P(("tm", "diag"))
    return jax.shard_map(
        on_device, mesh=mesh, in_specs=in_specs, out_specs=out_specs, check_vma=False
    )
```

time: 99 us -> 20.6 us (0.21)
  the two profiles are of different devices: /device:TPU:4 before, /device:TPU:0 now
where the time goes in v1:
time: 20.6 us; the launch traced here: 20.2 us
  starting transfers between devices  8.79 us (43%)
  Pallas kernels  6.38 us (31%)
  waiting for transfers between devices  2.59 us (13%)
  between operations  1.33 us (6%)
  local copies, waits for them, and re-layouts  0.62 us (3%)
  other arithmetic  0.53 us (3%)
    pallas_call x1, Pallas kernels, on_device(): pl.pallas_call(functools.partial(kernel, geo), out_shape=jax.ShapeDtypeSt...  6.38 us
    ppermute x2, starting transfers between devices, swapped(): return lax.ppermute(shard, axis, [(i, i ^ bit) for i in range(size)])  6.15 us
    ppermute x2, starting transfers between devices, shifted(): lax.ppermute(shard, axis, [(i, (i + by) % size) for i in range(size)])  2.64 us
    ppermute x2, waiting for transfers between devices, swapped(): return lax.ppermute(shard, axis, [(i, i ^ bit) for i in range(size)])  1.55 us
    ppermute x2, waiting for transfers between devices, shifted(): lax.ppermute(shard, axis, [(i, (i + by) % size) for i in range(size)])  1.04 us
    unnamed x4, local copies, waits for them, and re-layouts  0.62 us
    add x2, other arithmetic, group_offsets(): slots = slots + swapped(slots, 'diag', bit)  0.52 us
  transfers between devices with their start and end apart: 4, of which 3 were waited for; matrix products, arithmetic and copies ran while one was open for 3% of the time, Pallas kernels for 0%

profile of v1, /device:TPU:0, one launch (start us, length us, event | category | flops | bytes accessed | tf_op | source)
XLA Modules:
  0.0 20.2 jit_solution(10612277784359016509)
XLA Ops:
  0.7 3.1 %collective-permute-start = (s32[128]{0:T(128)S(1)}, s32[128]{0:T(128)S(1)}, u32[]{:S(2)}, u32[]{:S(2)}) collective-permute-start(s32[128]{0:T(128)S(1)} %compare_select_fusion), channel_id=1, source_target_pairs={{0,1},{1,0},{2,3},{3,2},{4,5},{5,4},{6,7},{7,6},{8,9},{9,8},{10,11... | collective-permute-start | bytes 1544 | tf_op jit(solution)/shard_map/ppermute | solution.py:29
  3.8 1.5 %collective-permute-done = s32[128]{0:T(128)S(1)} collective-permute-done((s32[128]{0:T(128)S(1)}, s32[128]{0:T(128)S(1)}, u32[]{:S(2)}, u32[]{:S(2)}) %collective-permute-start) | collective-permute-done | bytes 544 | tf_op jit(solution)/shard_map/ppermute | solution.py:29
  5.3 3.0 %collective-permute-start.1 = (s32[128]{0:T(128)S(1)}, s32[128]{0:T(128)S(1)}, u32[]{:S(2)}, u32[]{:S(2)}) collective-permute-start(s32[128]{0:T(128)S(1)} %fusion), channel_id=1, source_target_pairs={{0,2},{1,3},{2,0},{3,1},{4,6},{5,7},{6,4},{7,5},{8,10},{9,11},{10,... | collective-permute-start | bytes 1544 | tf_op jit(solution)/shard_map/ppermute | solution.py:29
  8.4 0.0 collective-permute-start.2
  8.4 2.6 %collective-permute-start.3 = (f32[16384]{0:T(1024)}, f32[16384]{0:T(1024)S(1)}, u32[]{:S(2)}, u32[]{:S(2)}) collective-permute-start(f32[16384]{0:T(1024)} %param.4), channel_id=1, source_target_pairs={{0,28},{4,0},{8,4},{12,8},{16,12},{20,16},{24,20},{28,24},{1,29},{... | collective-permute-start | bytes 196616 | tf_op jit(solution)/shard_map/ppermute | solution.py:24
  11.7 0.0 collective-permute-done.1
  11.7 0.5 %fusion.1.offs_ref = s32[128]{0:T(128)} fusion(s32[128]{0:T(128)S(1)} %collective-permute-done.1, s32[128]{0:T(128)S(1)} %collective-permute-done, s32[]{:T(128)} %bitcast.8, s32[]{:T(128)S(6)} %axis_index.12), kind=kLoop, calls=%fused_computation.2 | loop fusion | flops 512 | bytes 1544 | tf_op jit(solution)/shard_map/add | solution.py:37
  12.2 1.0 %collective-permute-done.2 = f32[16384]{0:T(1024)S(1)} collective-permute-done((f32[16384]{0:T(1024)}, f32[16384]{0:T(1024)S(1)}, u32[]{:S(2)}, u32[]{:S(2)}) %collective-permute-start.2) | collective-permute-done | bytes 65568 | tf_op jit(solution)/shard_map/ppermute | solution.py:24
  13.2 0.0 copy-start
  13.2 0.1 collective-permute-done.3
  13.2 0.0 copy-start.1
  13.2 0.5 %copy-done = f32[16384]{0:T(1024)} copy-done((f32[16384]{0:T(1024)}, f32[16384]{0:T(1024)S(1)}, u32[]{:S(2)}) %copy-start) | copy-done | bytes 65560
  13.8 0.1 copy-done.1
  13.9 6.4 %shard_map.46 = f32[32,128]{1,0:T(8,128)} custom-call(s32[128]{0:T(128)} %fusion.1.offs_ref, s32[1]{0:T(128)S(6)} %copy.6.excl_ref, f32[128,128]{1,0:T(8,128)} %bitcast.10, f32[128,128]{1,0:T(8,128)} %bitcast.9, f32[128,128]{1,0:T(8,128)} %bitcast.11, f32[2,128]{1,0:T(2,128)} %bitcast.12), custom_call_target="tpu_custom_call" | custom-call | tf_op jit(solution)/shard_map/pallas_call | solution.py:260
  (2 shorter events, 0.0 us)
Async XLA Ops:
  0.7 4.7 %collective-permute-start = (s32[128]{0:T(128)S(1)}, s32[128]{0:T(128)S(1)}, u32[]{:S(2)}, u32[]{:S(2)}) collective-permute-start(s32[128]{0:T(128)S(1)} %compare_select_fusion), channel_id=1, source_target_pairs={{0,1},{1,0},{2,3},{3,2},{4,5},{5,4},{6,7},{7,6},{8,9},{9,8},{10,11... | collective-permute-start | bytes 1544 | tf_op jit(solution)/shard_map/ppermute | solution.py:29
  5.3 6.3 %collective-permute-start.1 = (s32[128]{0:T(128)S(1)}, s32[128]{0:T(128)S(1)}, u32[]{:S(2)}, u32[]{:S(2)}) collective-permute-start(s32[128]{0:T(128)S(1)} %fusion), channel_id=1, source_target_pairs={{0,2},{1,3},{2,0},{3,1},{4,6},{5,7},{6,4},{7,5},{8,10},{9,11},{10,... | collective-permute-start | bytes 1544 | tf_op jit(solution)/shard_map/ppermute | solution.py:29
  8.4 4.8 %collective-permute-start.2 = (f32[16384]{0:T(1024)}, f32[16384]{0:T(1024)S(1)}, u32[]{:S(2)}, u32[]{:S(2)}) collective-permute-start(f32[16384]{0:T(1024)} %param.4), channel_id=1, source_target_pairs={{0,4},{4,8},{8,12},{12,16},{16,20},{20,24},{24,28},{28,0},{1,5},{5... | collective-permute-start | bytes 196616 | tf_op jit(solution)/shard_map/ppermute | solution.py:24
  8.4 4.9 %collective-permute-start.3 = (f32[16384]{0:T(1024)}, f32[16384]{0:T(1024)S(1)}, u32[]{:S(2)}, u32[]{:S(2)}) collective-permute-start(f32[16384]{0:T(1024)} %param.4), channel_id=1, source_target_pairs={{0,28},{4,0},{8,4},{12,8},{16,12},{20,16},{24,20},{28,24},{1,29},{... | collective-permute-start | bytes 196616 | tf_op jit(solution)/shard_map/ppermute | solution.py:24
  13.2 0.6 %copy-start = (f32[16384]{0:T(1024)}, f32[16384]{0:T(1024)S(1)}, u32[]{:S(2)}) copy-start(f32[16384]{0:T(1024)S(1)} %collective-permute-done.2) | copy-start | bytes 196612
  13.2 0.6 %copy-start.1 = (f32[16384]{0:T(1024)}, f32[16384]{0:T(1024)S(1)}, u32[]{:S(2)}) copy-start(f32[16384]{0:T(1024)S(1)} %collective-permute-done.3) | copy-start | bytes 196612

commit v2 on v1

--- a/solution.py
+++ b/solution.py
@@ -17,6 +17,8 @@
 XROWS = LANES + KB + M
 BIG = 1e30
 UNROLL = 8
+VMEM_LIMIT = 16 << 20
+COST_A = 1 << 23
 
 
 def shifted(shard, axis, by):
@@ -32,11 +34,13 @@
 def group_offsets(own):
     size = lax.axis_size("diag")
     slots = jnp.where(lax.iota(jnp.int32, LANES) == lax.axis_index("diag"), own[0], 0)
+    other = jnp.zeros_like(slots)
     bit = 1
     while bit < size:
-        slots = slots + swapped(slots, "diag", bit)
+        slots = slots + other
+        other = swapped(slots, "diag", bit)
         bit *= 2
-    return slots
+    return slots, other
 
 
 def split3(x):
@@ -55,12 +59,11 @@
     return out
 
 
-def kernel(geo, offs_ref, excl_ref, left_ref, own_ref, right_ref, tail_ref, out_ref,
-           ext, sums, text, stext, utext, xband, sband, uband, pband, xown, mown, best):
-    segrows, share_rows, back, nrows, groups, places = geo
+def prepare(geo, left_ref, own_ref, right_ref, tail_ref,
+            text, stext, utext, xown, mown, sown, ext, sums):
+    segrows, share_rows, back, groups, places = geo
     place = lax.axis_index("tm")
     diag = lax.axis_index("diag")
-    excl = excl_ref[0]
 
     ext[0:segrows, :] = left_ref[...]
     ext[segrows : 2 * segrows, :] = own_ref[...]
@@ -136,7 +139,16 @@
     for n in range(3):
         xown[n * LANES : (n + 1) * LANES, :] = own_rows(xt, n)
     mown[...] = own_rows(mt, 0)
-    spread_own = own_rows(st, 0)
+    sown[...] = own_rows(st, 0)
+
+
+def profile(geo, mine_ref, other_ref, excl_ref, text, stext, utext, xown, mown, sown, out_ref,
+            xband, sband, uband, pband, best):
+    segrows, share_rows, back, groups, places = geo
+    place = lax.axis_index("tm")
+    diag = lax.axis_index("diag")
+    excl = excl_ref[0]
+    offsets = mine_ref[...] + other_ref[...]
 
     lane8 = lax.broadcasted_iota(jnp.int32, (1, LANES), 1)
     sub8 = lax.broadcasted_iota(jnp.int32, (SUB, LANES), 0)
@@ -149,7 +161,7 @@
         lo = jnp.zeros((1, LANES), jnp.int32)
         xs = ss = us = None
         for g in range(groups):
-            off = offs_ref[g]
+            off = offsets[0, g]
             lag = off if way == 0 else -(off + (KB - 1))
             base = back * LANES + lag
             col = base // LANES
@@ -235,7 +247,7 @@
     while width < LANES:
         top = jnp.maximum(top, pltpu.roll(top, width, 1))
         width *= 2
-    distance = jnp.sqrt(jnp.maximum(1.0 - top * spread_own, 0.0))
+    distance = jnp.sqrt(jnp.maximum(1.0 - top * sown[...], 0.0))
     distance = jnp.where(top < -1e20, FILL, distance)
     out_ref[...] = distance.T[0:share_rows, :]
 
@@ -249,34 +261,50 @@
     share_rows = segrows // groups
     back = reach // LANES
     deepest = segrows - back + share_rows * (groups - 1)
-    geo = (segrows, share_rows, back, 2 * back + share_rows, groups, places)
+    geo = (segrows, share_rows, back, groups, places)
+    mine, other = group_offsets(diag_offsets)
     left = shifted(series, "tm", 1)
     right = shifted(series, "tm", -1)
-    offsets = group_offsets(diag_offsets)
     f32 = jnp.float32
     rows = lambda a: a.reshape(-1, LANES)
     smem = pl.BlockSpec(memory_space=pltpu.SMEM)
     vmem = pl.BlockSpec(memory_space=pltpu.VMEM)
-    out = pl.pallas_call(
-        functools.partial(kernel, geo),
-        out_shape=jax.ShapeDtypeStruct((share_rows, LANES), f32),
-        in_specs=[smem, smem, vmem, vmem, vmem, vmem],
-        out_specs=vmem,
+    tables = pl.pallas_call(
+        functools.partial(prepare, geo),
+        out_shape=[
+            jax.ShapeDtypeStruct((3, 5 * LANES, LANES), f32),
+            jax.ShapeDtypeStruct((3, 3 * LANES, LANES), f32),
+            jax.ShapeDtypeStruct((3, 3 * LANES, LANES), f32),
+            jax.ShapeDtypeStruct((3 * LANES, LANES), f32),
+            jax.ShapeDtypeStruct((LANES, LANES), f32),
+            jax.ShapeDtypeStruct((LANES, LANES), f32),
+        ],
+        in_specs=[vmem] * 4,
+        out_specs=[vmem] * 6,
         scratch_shapes=[
             pltpu.VMEM((max(3 * segrows, deepest + 2 * LANES), LANES), f32),
             pltpu.VMEM((2 * LANES, 2 * LANES), f32),
-            pltpu.VMEM((3, 5 * LANES, LANES), f32),
-            pltpu.VMEM((3, 3 * LANES, LANES), f32),
-            pltpu.VMEM((3, 3 * LANES, LANES), f32),
+        ],
+        compiler_params=pltpu.CompilerParams(vmem_limit_bytes=VMEM_LIMIT),
+        cost_estimate=pl.CostEstimate(flops=COST_A, bytes_accessed=1 << 20, transcendentals=0),
+        name="prepare",
+    )(rows(left), rows(series), rows(right), rows(tail))
+    out = pl.pallas_call(
+        functools.partial(profile, geo),
+        out_shape=jax.ShapeDtypeStruct((share_rows, LANES), f32),
+        in_specs=[vmem, vmem, smem] + [vmem] * 6,
+        out_specs=vmem,
+        scratch_shapes=[
             pltpu.VMEM((2, XROWS, LANES), f32),
             pltpu.VMEM((2, WROWS, LANES), f32),
             pltpu.VMEM((2, WROWS, LANES), f32),
             pltpu.VMEM((2, WROWS, LANES), f32),
-            pltpu.VMEM((3 * LANES, LANES), f32),
-            pltpu.VMEM((LANES, LANES), f32),
             pltpu.VMEM((LANES * SUB, LANES), f32),
         ],
-    )(offsets, exclusion, rows(left), rows(series), rows(right), rows(tail))
+        compiler_params=pltpu.CompilerParams(vmem_limit_bytes=VMEM_LIMIT),
+        cost_estimate=pl.CostEstimate(flops=1 << 24, bytes_accessed=1 << 20, transcendentals=0),
+        name="profile",
+    )(rows(mine), rows(other), exclusion, *tables)
     return out.reshape(-1)
 
 

time: 20.6 us -> 17.4 us (0.84)
  waiting for transfers between devices: 2.59 us -> 0.01 us
  local copies, waits for them, and re-layouts: 0.62 us -> 1.51 us
  other arithmetic: 0.53 us -> 0.01 us
  Pallas kernels: 6.38 us -> 5.87 us
  starting transfers between devices: 8.79 us -> 8.42 us
    ppermute x2, waiting for transfers between devices: 1.55 us -> 0.01 us  [swapped(): return lax.ppermute(shard, axis, [(i, i ^ bit) for i in range(size)])]
    ppermute x2, waiting for transfers between devices: 1.04 us -> 0.01 us  [shifted(): lax.ppermute(shard, axis, [(i, (i + by) % size) for i in range(size)])]
    unnamed x4, local copies, waits for them, and re-layouts: 0.62 us -> 1.51 us
    add x2 -> x1, other arithmetic: 0.52 us -> 0.01 us  [group_offsets(): slots = slots + other]
    pallas_call x1 -> x2, Pallas kernels: 6.38 us -> 5.87 us  [the longest x1 4.2 us: on_device(): pl.pallas_call(functools.partial(profile, geo), out_shape=jax.ShapeDtypeS...]
    ppermute x2, starting transfers between devices: 6.15 us -> 5.77 us  [swapped(): return lax.ppermute(shard, axis, [(i, i ^ bit) for i in range(size)])]
  transfers between devices with their start and end apart: 4 -> 4, of which waited for: 3 -> 0; matrix products, arithmetic and copies ran while one was open for 3% -> 0% of each run, Pallas kernels for 0% -> 10%
where the time goes in v2:
time: 17.4 us; the launch traced here: 17.2 us
  starting transfers between devices  8.42 us (48%)
  Pallas kernels  5.87 us (34%)
  local copies, waits for them, and re-layouts  1.51 us (9%)
  between operations  1.36 us (8%)
    ppermute x2, starting transfers between devices, swapped(): return lax.ppermute(shard, axis, [(i, i ^ bit) for i in range(size)])  5.77 us
    pallas_call x1, Pallas kernels, on_device(): pl.pallas_call(functools.partial(profile, geo), out_shape=jax.ShapeDtypeS...  4.2 us
    ppermute x2, starting transfers between devices, shifted(): lax.ppermute(shard, axis, [(i, (i + by) % size) for i in range(size)])  2.64 us
    pallas_call x1, Pallas kernels, on_device(): pl.pallas_call(functools.partial(prepare, geo), out_shape=[jax.ShapeDtype...  1.66 us
    unnamed x4, local copies, waits for them, and re-layouts  1.51 us
  transfers between devices with their start and end apart: 4, of which 0 were waited for; matrix products, arithmetic and copies ran while one was open for 0% of the time, Pallas kernels for 10%

profile of v2, /device:TPU:0, one launch (start us, length us, event | category | flops | bytes accessed | tf_op | source)
XLA Modules:
  0.0 17.2 jit_solution(14010162269109624059)
XLA Ops:
  0.7 3.1 %collective-permute-start = (s32[128]{0:T(128)S(1)}, s32[128]{0:T(128)S(1)}, u32[]{:S(2)}, u32[]{:S(2)}) collective-permute-start(s32[128]{0:T(128)S(1)} %compare_select_fusion), channel_id=1, source_target_pairs={{0,1},{1,0},{2,3},{3,2},{4,5},{5,4},{6,7},{7,6},{8,9},{9,8},{10,11... | collective-permute-start | bytes 1544 | tf_op jit(solution)/shard_map/ppermute | solution.py:31
  3.8 0.0 collective-permute-start.2
  3.8 2.6 %collective-permute-start.3 = (f32[16384]{0:T(1024)}, f32[16384]{0:T(1024)S(1)}, u32[]{:S(2)}, u32[]{:S(2)}) collective-permute-start(f32[16384]{0:T(1024)} %param.4), channel_id=1, source_target_pairs={{0,28},{4,0},{8,4},{12,8},{16,12},{20,16},{24,20},{28,24},{1,29},{... | collective-permute-start | bytes 196616 | tf_op jit(solution)/shard_map/ppermute | solution.py:26
  7.1 0.0 collective-permute-done
  7.1 2.7 %collective-permute-start.1 = (s32[128]{0:T(128)S(1)}, s32[128]{0:T(128)S(1)}, u32[]{:S(2)}, u32[]{:S(2)}) collective-permute-start(s32[128]{0:T(128)S(1)} %fusion), channel_id=1, source_target_pairs={{0,2},{1,3},{2,0},{3,1},{4,6},{5,7},{6,4},{7,5},{8,10},{9,11},{10,... | collective-permute-start | bytes 1544 | tf_op jit(solution)/shard_map/ppermute | solution.py:31
  9.8 0.0 collective-permute-done.2
  9.8 0.0 collective-permute-done.3
  9.8 0.0 copy-start.1
  9.8 0.7 %copy-done.1 = f32[256]{0:T(256)S(1)} copy-done((f32[256]{0:T(256)S(1)}, f32[256]{0:T(256)}, u32[]{:S(2)}) %copy-start.1) | copy-done | bytes 1048
  10.5 0.0 copy-start
  10.5 0.8 %copy-done = f32[16384]{0:T(1024)S(1)} copy-done((f32[16384]{0:T(1024)S(1)}, f32[16384]{0:T(1024)}, u32[]{:S(2)}) %copy-start) | copy-done | bytes 65560
  11.3 1.7 %prepare.1 = (f32[3,640,128]{2,1,0:T(8,128)S(1)}, f32[3,384,128]{2,1,0:T(8,128)S(1)}, f32[3,384,128]{2,1,0:T(8,128)S(1)}, f32[384,128]{1,0:T(8,128)S(1)}, f32[12...) custom-call(f32[128,128]{1,0:T(8,128)S(1)} %bitcast.13, f32[128,128]{1,0:T(8,128)S(1)} %bitcast.12, f32[128,128]{1,0:T(8,128)S(1)} %bitcast.14, ...), custom_call_target="tpu_custom_call" | custom-call | flops 8388608 | bytes 1048576 | tf_op jit(solution)/shard_map/prepare/pallas_call | solution.py:272
  13.0 0.0 collective-permute-done.1
  13.0 4.2 %profile.1 = f32[32,128]{1,0:T(8,128)} custom-call(s32[1,128]{1,0:T(1,128)S(1)} %fusion.1.mine_ref, s32[1,128]{1,0:T(1,128)S(1)} %bitcast.16, s32[1]{0:T(128)S(6)} %copy.6.excl_ref, f32[3,640,128]{2,1,0:T(8,128)S(1)} %get-tuple-element.11.text, f32[3,384,128]{2,1,0:T(8,128)S(1)} %get-tuple-element.12.stext, f32[3,384,128]{2,1,0:T(8,128)S(1)} %get-tuple-element.13.utext, ...), custom_call_target="tpu_custom_call" | custom-call | flops 16777216 | bytes 1048576 | tf_op jit(solution)/shard_map/profile/pallas_call | solution.py:292
  (3 shorter events, 0.0 us)
Async XLA Ops:
  0.7 6.4 %collective-permute-start = (s32[128]{0:T(128)S(1)}, s32[128]{0:T(128)S(1)}, u32[]{:S(2)}, u32[]{:S(2)}) collective-permute-start(s32[128]{0:T(128)S(1)} %compare_select_fusion), channel_id=1, source_target_pairs={{0,1},{1,0},{2,3},{3,2},{4,5},{5,4},{6,7},{7,6},{8,9},{9,8},{10,11... | collective-permute-start | bytes 1544 | tf_op jit(solution)/shard_map/ppermute | solution.py:31
  3.8 6.0 %collective-permute-start.2 = (f32[16384]{0:T(1024)}, f32[16384]{0:T(1024)S(1)}, u32[]{:S(2)}, u32[]{:S(2)}) collective-permute-start(f32[16384]{0:T(1024)} %param.4), channel_id=1, source_target_pairs={{0,4},{4,8},{8,12},{12,16},{16,20},{20,24},{24,28},{28,0},{1,5},{5... | collective-permute-start | bytes 196616 | tf_op jit(solution)/shard_map/ppermute | solution.py:26
  3.8 6.0 %collective-permute-start.3 = (f32[16384]{0:T(1024)}, f32[16384]{0:T(1024)S(1)}, u32[]{:S(2)}, u32[]{:S(2)}) collective-permute-start(f32[16384]{0:T(1024)} %param.4), channel_id=1, source_target_pairs={{0,28},{4,0},{8,4},{12,8},{16,12},{20,16},{24,20},{28,24},{1,29},{... | collective-permute-start | bytes 196616 | tf_op jit(solution)/shard_map/ppermute | solution.py:26
  7.1 5.9 %collective-permute-start.1 = (s32[128]{0:T(128)S(1)}, s32[128]{0:T(128)S(1)}, u32[]{:S(2)}, u32[]{:S(2)}) collective-permute-start(s32[128]{0:T(128)S(1)} %fusion), channel_id=1, source_target_pairs={{0,2},{1,3},{2,0},{3,1},{4,6},{5,7},{6,4},{7,5},{8,10},{9,11},{10,... | collective-permute-start | bytes 1544 | tf_op jit(solution)/shard_map/ppermute | solution.py:31
  9.8 0.7 %copy-start.1 = (f32[256]{0:T(256)S(1)}, f32[256]{0:T(256)}, u32[]{:S(2)}) copy-start(f32[256]{0:T(256)} %param.5) | copy-start | bytes 3076
  10.5 0.8 %copy-start = (f32[16384]{0:T(1024)S(1)}, f32[16384]{0:T(1024)}, u32[]{:S(2)}) copy-start(f32[16384]{0:T(1024)} %param.4) | copy-start | bytes 196612

commit v3 on v2

--- a/solution.py
+++ b/solution.py
@@ -19,28 +19,25 @@
 UNROLL = 8
 VMEM_LIMIT = 16 << 20
 COST_A = 1 << 23
-
-
-def shifted(shard, axis, by):
+COST_STAGE = 1 << 21
+
+
+def swapped(shard, axis, partner):
     size = lax.axis_size(axis)
-    return lax.ppermute(shard, axis, [(i, (i + by) % size) for i in range(size)])
-
-
-def swapped(shard, axis, bit):
-    size = lax.axis_size(axis)
-    return lax.ppermute(shard, axis, [(i, i ^ bit) for i in range(size)])
-
-
-def group_offsets(own):
+    return lax.ppermute(shard, axis, [(i, partner(i) % size) for i in range(size)])
+
+
+def group_offsets(own, exclusion):
     size = lax.axis_size("diag")
-    slots = jnp.where(lax.iota(jnp.int32, LANES) == lax.axis_index("diag"), own[0], 0)
+    lanes = lax.iota(jnp.int32, LANES)
+    slots = jnp.where(lanes == lax.axis_index("diag"), own[0], 0)
     other = jnp.zeros_like(slots)
     bit = 1
     while bit < size:
         slots = slots + other
-        other = swapped(slots, "diag", bit)
+        other = swapped(slots, "diag", lambda i: i ^ bit)
         bit *= 2
-    return slots, other
+    return slots + jnp.where(lanes == LANES - 1, exclusion[0], 0), other
 
 
 def split3(x):
@@ -59,15 +56,36 @@
     return out
 
 
-def prepare(geo, left_ref, own_ref, right_ref, tail_ref,
+def stage(series_ref, tail_ref, series_out, tail_out, sems):
+    copies = [
+        pltpu.make_async_copy(series_ref, series_out, sems.at[0]),
+        pltpu.make_async_copy(tail_ref, tail_out, sems.at[1]),
+    ]
+    for copy in copies:
+        copy.start()
+    for copy in copies:
+        copy.wait()
+
+
+def prepare(geo, near_ref, own_ref, far_ref, tail_ref,
             text, stext, utext, xown, mown, sown, ext, sums):
     segrows, share_rows, back, groups, places = geo
     place = lax.axis_index("tm")
     diag = lax.axis_index("diag")
 
-    ext[0:segrows, :] = left_ref[...]
+    odd = lax.rem(place, 2) == 1
+    last = place == places - 1
     ext[segrows : 2 * segrows, :] = own_ref[...]
-    last = place == places - 1
+
+    @pl.when(odd)
+    def _():
+        ext[0:segrows, :] = near_ref[...]
+        ext[2 * segrows : 3 * segrows, :] = far_ref[...]
+
+    @pl.when(jnp.logical_not(odd))
+    def _():
+        ext[0:segrows, :] = far_ref[...]
+        ext[2 * segrows : 3 * segrows, :] = near_ref[...]
 
     @pl.when(last)
     def _():
@@ -77,10 +95,6 @@
             (segrows - tail_rows, LANES), jnp.float32
         )
 
-    @pl.when(jnp.logical_not(last))
-    def _():
-        ext[2 * segrows : 3 * segrows, :] = right_ref[...]
-
     if ext.shape[0] > 3 * segrows:
         ext[3 * segrows :, :] = jnp.zeros((ext.shape[0] - 3 * segrows, LANES), jnp.float32)
     first_row = pl.multiple_of(segrows - back + share_rows * diag, SUB)
@@ -142,13 +156,13 @@
     sown[...] = own_rows(st, 0)
 
 
-def profile(geo, mine_ref, other_ref, excl_ref, text, stext, utext, xown, mown, sown, out_ref,
+def profile(geo, mine_ref, other_ref, text, stext, utext, xown, mown, sown, out_ref,
             xband, sband, uband, pband, best):
     segrows, share_rows, back, groups, places = geo
     place = lax.axis_index("tm")
     diag = lax.axis_index("diag")
-    excl = excl_ref[0]
     offsets = mine_ref[...] + other_ref[...]
+    excl = mine_ref[0, LANES - 1]
 
     lane8 = lax.broadcasted_iota(jnp.int32, (1, LANES), 1)
     sub8 = lax.broadcasted_iota(jnp.int32, (SUB, LANES), 0)
@@ -262,13 +276,27 @@
     back = reach // LANES
     deepest = segrows - back + share_rows * (groups - 1)
     geo = (segrows, share_rows, back, groups, places)
-    mine, other = group_offsets(diag_offsets)
-    left = shifted(series, "tm", 1)
-    right = shifted(series, "tm", -1)
     f32 = jnp.float32
     rows = lambda a: a.reshape(-1, LANES)
-    smem = pl.BlockSpec(memory_space=pltpu.SMEM)
+    held = lambda a: pltpu.with_memory_space_constraint(a, pltpu.HBM)
     vmem = pl.BlockSpec(memory_space=pltpu.VMEM)
+    hbm = pl.BlockSpec(memory_space=pltpu.HBM)
+    mine, other = group_offsets(diag_offsets, exclusion)
+    own, end = pl.pallas_call(
+        stage,
+        out_shape=[
+            jax.ShapeDtypeStruct((segrows, LANES), f32),
+            jax.ShapeDtypeStruct((M // LANES, LANES), f32),
+        ],
+        in_specs=[hbm] * 2,
+        out_specs=[vmem] * 2,
+        scratch_shapes=[pltpu.SemaphoreType.DMA((2,))],
+        compiler_params=pltpu.CompilerParams(vmem_limit_bytes=VMEM_LIMIT),
+        cost_estimate=pl.CostEstimate(flops=COST_STAGE, bytes_accessed=1 << 17, transcendentals=0),
+        name="stage",
+    )(held(rows(series)), held(rows(tail)))
+    far = swapped(own, "tm", lambda i: i + 1 if i % 2 else i - 1)
+    near = swapped(own, "tm", lambda i: i ^ 1)
     tables = pl.pallas_call(
         functools.partial(prepare, geo),
         out_shape=[
@@ -288,11 +316,11 @@
         compiler_params=pltpu.CompilerParams(vmem_limit_bytes=VMEM_LIMIT),
         cost_estimate=pl.CostEstimate(flops=COST_A, bytes_accessed=1 << 20, transcendentals=0),
         name="prepare",
-    )(rows(left), rows(series), rows(right), rows(tail))
+    )(near, own, far, end)
     out = pl.pallas_call(
         functools.partial(profile, geo),
         out_shape=jax.ShapeDtypeStruct((share_rows, LANES), f32),
-        in_specs=[vmem, vmem, smem] + [vmem] * 6,
+        in_specs=[vmem] * 8,
         out_specs=vmem,
         scratch_shapes=[
             pltpu.VMEM((2, XROWS, LANES), f32),
@@ -304,7 +332,7 @@
         compiler_params=pltpu.CompilerParams(vmem_limit_bytes=VMEM_LIMIT),
         cost_estimate=pl.CostEstimate(flops=1 << 24, bytes_accessed=1 << 20, transcendentals=0),
         name="profile",
-    )(rows(mine), rows(other), exclusion, *tables)
+    )(rows(mine), rows(other), *tables)
     return out.reshape(-1)
 
 

time: 17.4 us -> 16.8 us (0.966)
  local copies, waits for them, and re-layouts: 1.51 us -> 0 us
  Pallas kernels: 5.87 us -> 6.68 us
  waiting for transfers between devices: 0.01 us -> 0.2 us
    unnamed x4 -> x0, local copies, waits for them, and re-layouts: 1.51 us -> none
    pallas_call x0 -> x1, Pallas kernels: none -> 0.86 us  [on_device(): pl.pallas_call(stage, out_shape=[jax.ShapeDtypeStruct((segrows, LANES), f...]
    ppermute x4, waiting for transfers between devices: 0.01 us -> 0.2 us  [swapped(): lax.ppermute(shard, axis, [(i, partner(i) % size) for i in range(size)])]
  transfers between devices with their start and end apart: 4 -> 4, of which waited for: 0 -> 1; matrix products, arithmetic and copies ran while one was open for 0% -> 0% of each run, Pallas kernels for 10% -> 15%
where the time goes in v3:
time: 16.8 us; the launch traced here: 16.6 us
  starting transfers between devices  8.39 us (50%)
  Pallas kernels  6.68 us (40%)
  between operations  1.35 us (8%)
  waiting for transfers between devices  0.2 us (1%)
    ppermute x4, starting transfers between devices, swapped(): lax.ppermute(shard, axis, [(i, partner(i) % size) for i in range(size)])  8.39 us
    pallas_call x1, Pallas kernels, on_device(): pl.pallas_call(functools.partial(profile, geo), out_shape=jax.ShapeDtypeS...  4.14 us
    pallas_call x1, Pallas kernels, on_device(): pl.pallas_call(functools.partial(prepare, geo), out_shape=[jax.ShapeDtype...  1.68 us
    pallas_call x1, Pallas kernels, on_device(): pl.pallas_call(stage, out_shape=[jax.ShapeDtypeStruct((segrows, LANES), f...  0.86 us
  transfers between devices with their start and end apart: 4, of which 1 were waited for; matrix products, arithmetic and copies ran while one was open for 0% of the time, Pallas kernels for 15%

profile of v3, /device:TPU:0, one launch (start us, length us, event | category | flops | bytes accessed | tf_op | source)
XLA Modules:
  0.0 16.6 jit_solution(2409554507478799674)
XLA Ops:
  0.7 3.1 %collective-permute-start = (s32[128]{0:T(128)S(1)}, s32[128]{0:T(128)S(1)}, u32[]{:S(2)}, u32[]{:S(2)}) collective-permute-start(s32[128]{0:T(128)S(1)} %compare_select_fusion.1), channel_id=1, source_target_pairs={{0,1},{1,0},{2,3},{3,2},{4,5},{5,4},{6,7},{7,6},{8,9},{9,8},{10,11... | collective-permute-start | bytes 1544 | tf_op jit(solution)/shard_map/ppermute | solution.py:27
  3.8 0.9 %stage.1 = (f32[128,128]{1,0:T(8,128)S(1)}, f32[2,128]{1,0:T(2,128)S(1)}) custom-call(f32[128,128]{1,0:T(8,128)} %bitcast.12, f32[2,128]{1,0:T(2,128)} %bitcast.13), custom_call_target="tpu_custom_call" | custom-call | flops 2097152 | bytes 131072 | tf_op jit(solution)/shard_map/stage/pallas_call | solution.py:285
  4.6 0.1 collective-permute-start.2
  4.7 2.5 %collective-permute-start.3 = (f32[128,128]{1,0:T(8,128)S(1)}, f32[128,128]{1,0:T(8,128)S(1)}, u32[]{:S(2)}, u32[]{:S(2)}) collective-permute-start(f32[128,128]{1,0:T(8,128)S(1)} %get-tuple-element.13.own_ref), channel_id=1, source_target_pairs={{0,28},{4,8},{8,4},{12,16},{16,12},{20,24},{24,20},{28,0},{1,29},{... | collective-permute-start | bytes 196616 | tf_op jit(solution)/shard_map/ppermute | solution.py:27
  7.9 0.0 collective-permute-done
  8.0 2.7 %collective-permute-start.1 = (s32[128]{0:T(128)S(1)}, s32[128]{0:T(128)S(1)}, u32[]{:S(2)}, u32[]{:S(2)}) collective-permute-start(s32[128]{0:T(128)S(1)} %get-tuple-element.22), channel_id=1, source_target_pairs={{0,2},{1,3},{2,0},{3,1},{4,6},{5,7},{6,4},{7,5},{8,10},{9,11},{10,... | collective-permute-start | bytes 1544 | tf_op jit(solution)/shard_map/ppermute | solution.py:27
  10.6 0.0 collective-permute-done.2.near_ref
  10.6 0.0 collective-permute-done.3.far_ref
  10.6 1.7 %prepare.1 = (f32[3,640,128]{2,1,0:T(8,128)S(1)}, f32[3,384,128]{2,1,0:T(8,128)S(1)}, f32[3,384,128]{2,1,0:T(8,128)S(1)}, f32[384,128]{1,0:T(8,128)S(1)}, f32[12...) custom-call(f32[128,128]{1,0:T(8,128)S(1)} %collective-permute-done.2.near_ref, f32[128,128]{1,0:T(8,128)S(1)} %get-tuple-element.13.own_ref, ...), custom_call_target="tpu_custom_call" | custom-call | flops 8388608 | bytes 1048576 | tf_op jit(solution)/shard_map/prepare/pallas_call | solution.py:300
  12.3 0.2 %collective-permute-done.1 = s32[128]{0:T(128)S(1)} collective-permute-done((s32[128]{0:T(128)S(1)}, s32[128]{0:T(128)S(1)}, u32[]{:S(2)}, u32[]{:S(2)}) %collective-permute-start.1) | collective-permute-done | bytes 544 | tf_op jit(solution)/shard_map/ppermute | solution.py:27
  12.5 4.1 %profile.1 = f32[32,128]{1,0:T(8,128)} custom-call(s32[1,128]{1,0:T(1,128)S(1)} %get-tuple-element.21.mine_ref, s32[1,128]{1,0:T(1,128)S(1)} %bitcast.11, f32[3,640,128]{2,1,0:T(8,128)S(1)} %get-tuple-element.15.text, f32[3,384,128]{2,1,0:T(8,128)S(1)} %get-tuple-element.16.stext, f32[3,384,128]{2,1,0:T(8,128)S(1)} %get-tuple-element.17.utext, ...), custom_call_target="tpu_custom_call" | custom-call | flops 16777216 | bytes 1048576 | tf_op jit(solution)/shard_map/profile/pallas_call | solution.py:320
  (2 shorter events, 0.0 us)
Async XLA Ops:
  0.7 7.3 %collective-permute-start = (s32[128]{0:T(128)S(1)}, s32[128]{0:T(128)S(1)}, u32[]{:S(2)}, u32[]{:S(2)}) collective-permute-start(s32[128]{0:T(128)S(1)} %compare_select_fusion.1), channel_id=1, source_target_pairs={{0,1},{1,0},{2,3},{3,2},{4,5},{5,4},{6,7},{7,6},{8,9},{9,8},{10,11... | collective-permute-start | bytes 1544 | tf_op jit(solution)/shard_map/ppermute | solution.py:27
  4.6 6.0 %collective-permute-start.2 = (f32[128,128]{1,0:T(8,128)S(1)}, f32[128,128]{1,0:T(8,128)S(1)}, u32[]{:S(2)}, u32[]{:S(2)}) collective-permute-start(f32[128,128]{1,0:T(8,128)S(1)} %get-tuple-element.13.own_ref), channel_id=1, source_target_pairs={{0,4},{4,0},{8,12},{12,8},{16,20},{20,16},{24,28},{28,24},{1,5},{5... | collective-permute-start | bytes 196616 | tf_op jit(solution)/shard_map/ppermute | solution.py:27
  4.7 5.9 %collective-permute-start.3 = (f32[128,128]{1,0:T(8,128)S(1)}, f32[128,128]{1,0:T(8,128)S(1)}, u32[]{:S(2)}, u32[]{:S(2)}) collective-permute-start(f32[128,128]{1,0:T(8,128)S(1)} %get-tuple-element.13.own_ref), channel_id=1, source_target_pairs={{0,28},{4,8},{8,4},{12,16},{16,12},{20,24},{24,20},{28,0},{1,29},{... | collective-permute-start | bytes 196616 | tf_op jit(solution)/shard_map/ppermute | solution.py:27
  8.0 4.5 %collective-permute-start.1 = (s32[128]{0:T(128)S(1)}, s32[128]{0:T(128)S(1)}, u32[]{:S(2)}, u32[]{:S(2)}) collective-permute-start(s32[128]{0:T(128)S(1)} %get-tuple-element.22), channel_id=1, source_target_pairs={{0,2},{1,3},{2,0},{3,1},{4,6},{5,7},{6,4},{7,5},{8,10},{9,11},{10,... | collective-permute-start | bytes 1544 | tf_op jit(solution)/shard_map/ppermute | solution.py:27

commit v4 on v3

v4 whole, which is shorter than its diff:
```python
import functools

import jax
import jax.numpy as jnp
from jax import lax
from jax.experimental import pallas as pl
from jax.experimental.pallas import tpu as pltpu
from jax.sharding import PartitionSpec as P

M = 256
KB = 32
FILL = 1e30
LANES = 128
SUB = 8
STEP = KB // SUB
BROWS = M + KB
BIG = 1e30
UNROLL = 8
VMEM_LIMIT = 16 << 20
COST_A = 1 << 23
COST_STAGE = 1 << 21


def swapped(shard, axis, partner):
    size = lax.axis_size(axis)
    return lax.ppermute(shard, axis, [(i, partner(i) % size) for i in range(size)])


def group_offsets(own, exclusion):
    size = lax.axis_size("diag")
    lanes = lax.iota(jnp.int32, LANES)
    slots = jnp.where(lanes == lax.axis_index("diag"), own[0], 0)
    other = jnp.zeros_like(slots)
    bit = 1
    while bit < size:
        slots = slots + other
        other = swapped(slots, "diag", lambda i: i ^ bit)
        bit *= 2
    return slots + jnp.where(lanes == LANES - 1, exclusion[0], 0), other


def split3(x):
    hi = x.astype(jnp.bfloat16)
    rest = x - hi.astype(jnp.float32)
    mid = rest.astype(jnp.bfloat16)
    low = (rest - mid.astype(jnp.float32)).astype(jnp.bfloat16)
    return hi, mid, low


def window_pieces(x, ones):
    out = None
    for piece in split3(x):
        part = jnp.dot(piece, ones, preferred_element_type=jnp.float32)
        out = part if out is None else out + part
    return out


def stage(series_ref, tail_ref, series_out, tail_out, sems):
    copies = [
        pltpu.make_async_copy(series_ref, series_out, sems.at[0]),
        pltpu.make_async_copy(tail_ref, tail_out, sems.at[1]),
    ]
    for copy in copies:
        copy.start()
    for copy in copies:
        copy.wait()


def prepare(geo, near_ref, own_ref, far_ref, tail_ref,
            points, fall, rise, spreads, own_points, own_fall, own_rise, ext, sums):
    segrows, share_rows, back, groups, places = geo
    place = lax.axis_index("tm")
    diag = lax.axis_index("diag")

    odd = lax.rem(place, 2) == 1
    last = place == places - 1
    ext[segrows : 2 * segrows, :] = own_ref[...]

    @pl.when(odd)
    def _():
        ext[0:segrows, :] = near_ref[...]
        ext[2 * segrows : 3 * segrows, :] = far_ref[...]

    @pl.when(jnp.logical_not(odd))
    def _():
        ext[0:segrows, :] = far_ref[...]
        ext[2 * segrows : 3 * segrows, :] = near_ref[...]

    @pl.when(last)
    def _():
        tail_rows = M // LANES
        ext[2 * segrows : 2 * segrows + tail_rows, :] = tail_ref[...]
        ext[2 * segrows + tail_rows : 3 * segrows, :] = jnp.zeros(
            (segrows - tail_rows, LANES), jnp.float32
        )

    if ext.shape[0] > 3 * segrows:
        ext[3 * segrows :, :] = jnp.zeros((ext.shape[0] - 3 * segrows, LANES), jnp.float32)
    first_row = pl.multiple_of(segrows - back + share_rows * diag, SUB)
    points[...] = ext[pl.ds(first_row, 2 * LANES), :]

    rid = lax.broadcasted_iota(jnp.int32, (LANES, 2 * LANES), 0)
    cid = lax.broadcasted_iota(jnp.int32, (LANES, 2 * LANES), 1)
    ones = jnp.where(
        cid < LANES, (rid >= cid).astype(jnp.float32), (rid < cid - LANES).astype(jnp.float32)
    ).astype(jnp.bfloat16)
    held = 2 * LANES - SUB

    def windows(values):
        sums[...] = window_pieces(values, ones)
        return (
            sums[0:held, 0:LANES]
            + (sums[1 : held + 1, 0:LANES] + sums[1 : held + 1, LANES:])
            + sums[2 : held + 2, LANES:]
        )

    x = points[...]
    mean = windows(x) * (1.0 / M)
    second = windows(x * x) * (1.0 / M)
    here = points[0:held, :]
    there = points[2 : held + 2, :]
    change = there - here
    pad = jnp.zeros((SUB, LANES), jnp.float32)
    spreads[0:held, :] = lax.rsqrt(second - mean * mean + 1e-05)
    fall[0:held, :] = 0.5 * change
    rise[0:held, :] = (there + here) - 2.0 * mean - change * (1.0 / M)
    for ref in (spreads, fall, rise):
        ref[held:, :] = pad

    chunks = share_rows // 2

    def own_rows(ref):
        halves = []
        for half in range(2):
            rows = ref[pl.ds(back + half, chunks, stride=2), :]
            halves.append(jnp.concatenate([rows] * (LANES // chunks), axis=0).T)
        return jnp.concatenate(halves, axis=0)

    turned = own_rows(points)
    own_points[...] = turned - jnp.sum(turned, axis=0, keepdims=True) * (1.0 / M)
    own_fall[...] = own_rows(fall)
    own_rise[...] = own_rows(rise)


def profile(geo, mine_ref, other_ref, points, fall, rise, spreads, own_points, own_fall, own_rise,
            out_ref, moved, xband, fband, rband, sband, pband, best):
    segrows, share_rows, back, groups, places = geo
    place = lax.axis_index("tm")
    diag = lax.axis_index("diag")
    offsets = mine_ref[...] + other_ref[...]
    excl = mine_ref[0, LANES - 1]
    chunks = share_rows // 2

    lane = lax.broadcasted_iota(jnp.int32, (1, LANES), 1)
    sub = lax.broadcasted_iota(jnp.int32, (SUB, LANES), 0)
    lags, bases = [], []
    for way in range(2):
        for g in range(groups):
            off = offsets[0, g]
            lags.append(off if way == 0 else -(off + (KB - 1)))
    first_lag = jnp.zeros((1, LANES), jnp.int32)
    for j, lag in enumerate(lags):
        first_lag = jnp.where(lane >= chunks * j, lag, first_lag)
    rows = moved.shape[1]
    for ref, out in ((points, xband), (spreads, sband), (fall, fband), (rise, rband)):
        parts = [[] for _ in range(3)]
        for j, lag in enumerate(lags):
            base = back * LANES + lag
            row = base // LANES
            inner = base - row * LANES
            turn = lax.rem(LANES - inner, LANES)
            moved[j] = pltpu.roll(ref[pl.ds(row, rows), :], turn, 1)
            near = lane < LANES - inner
            for q in range(3):
                parts[q].append(
                    jnp.where(
                        near,
                        moved[j, pl.ds(q, chunks, stride=2), :],
                        moved[j, pl.ds(q + 1, chunks, stride=2), :],
                    )
                )
        for q in range(3):
            turned = jnp.concatenate(parts[q], axis=0).T
            out[q * LANES : min((q + 1) * LANES, BROWS), :] = turned[0 : min(LANES, BROWS - q * LANES)]
    limit = places * segrows * LANES
    own_start = (place * segrows + share_rows * diag) * LANES
    position = own_start + (lane & (chunks - 1)) * M + first_lag
    position = position + lax.broadcasted_iota(jnp.int32, (BROWS, LANES), 0)
    pband[...] = jnp.where((position >= 0) & (position < limit), BIG, -BIG)

    def band(ref, start):
        return ref[pl.ds(start, SUB, stride=STEP), :]

    def row(ref, i):
        return ref[pl.ds(i, SUB, stride=0), :]

    def first(step, totals):
        totals = list(totals)
        for u in range(UNROLL):
            i = step * UNROLL + u
            xi = row(own_points, i)
            for s in range(STEP):
                c = s + STEP * (u % 2)
                totals[c] = totals[c] + xi * band(xband, i + s)
        return tuple(totals)

    zero = jnp.zeros((SUB, LANES), jnp.float32)
    totals = lax.fori_loop(0, M // UNROLL, first, (zero,) * (2 * STEP))
    start = tuple(
        jnp.where(
            jnp.abs(first_lag + STEP * sub + s) < excl, -BIG, totals[s] + totals[s + STEP]
        )
        for s in range(STEP)
    )

    def advance(step, covs):
        covs = list(covs)
        for u in range(UNROLL):
            i = step * UNROLL + u
            fi = row(own_fall, i)
            ri = row(own_rise, i)
            top = None
            for s in range(STEP):
                value = jnp.minimum(covs[s] * band(sband, i + s), band(pband, i + s))
                top = value if top is None else jnp.maximum(top, value)
                covs[s] = covs[s] + (fi * band(rband, i + s) + ri * band(fband, i + s))
            best[pl.ds(pl.multiple_of(i * SUB, SUB), SUB), :] = top
        return tuple(covs)

    lax.fori_loop(0, M // UNROLL, advance, start)

    for half in range(2):
        blocks = []
        for block in range(LANES // SUB):
            top = None
            for h in range(SUB):
                at = (half * LANES + block * SUB) * SUB + h
                part = best[pl.ds(at, SUB, stride=SUB), :]
                top = part if top is None else jnp.maximum(top, part)
            blocks.append(top)
        turned = jnp.concatenate(blocks, axis=0).T
        top = turned[0:chunks]
        for j in range(1, 2 * groups):
            top = jnp.maximum(top, turned[chunks * j : chunks * (j + 1)])
        spread = spreads[pl.ds(back + half, chunks, stride=2), :]
        distance = jnp.sqrt(jnp.maximum(1.0 - top * (spread * (1.0 / M)), 0.0))
        out_ref[pl.ds(half, chunks, stride=2), :] = jnp.where(top < -1e20, FILL, distance)


def on_device(series, tail, diag_offsets, exclusion):
    segment = series.shape[0]
    groups = lax.axis_size("diag")
    places = lax.axis_size("tm")
    reach = segment // 2 + segment // 4
    segrows = segment // LANES
    share_rows = segrows // groups
    back = reach // LANES
    deepest = segrows - back + share_rows * (groups - 1)
    geo = (segrows, share_rows, back, groups, places)
    f32 = jnp.float32
    rows = lambda a: a.reshape(-1, LANES)
    held = lambda a: pltpu.with_memory_space_constraint(a, pltpu.HBM)
    vmem = pl.BlockSpec(memory_space=pltpu.VMEM)
    hbm = pl.BlockSpec(memory_space=pltpu.HBM)
    mine, other = group_offsets(diag_offsets, exclusion)
    own, end = pl.pallas_call(
        stage,
        out_shape=[
            jax.ShapeDtypeStruct((segrows, LANES), f32),
            jax.ShapeDtypeStruct((M // LANES, LANES), f32),
        ],
        in_specs=[hbm] * 2,
        out_specs=[vmem] * 2,
        scratch_shapes=[pltpu.SemaphoreType.DMA((2,))],
        compiler_params=pltpu.CompilerParams(vmem_limit_bytes=VMEM_LIMIT),
        cost_estimate=pl.CostEstimate(flops=COST_STAGE, bytes_accessed=1 << 17, transcendentals=0),
        name="stage",
    )(held(rows(series)), held(rows(tail)))
    far = swapped(own, "tm", lambda i: i + 1 if i % 2 else i - 1)
    near = swapped(own, "tm", lambda i: i ^ 1)
    table = jax.ShapeDtypeStruct((2 * LANES, LANES), f32)
    tables = pl.pallas_call(
        functools.partial(prepare, geo),
        out_shape=[table] * 7,
        in_specs=[vmem] * 4,
        out_specs=[vmem] * 7,
        scratch_shapes=[
            pltpu.VMEM((max(3 * segrows, deepest + 2 * LANES), LANES), f32),
            pltpu.VMEM((2 * LANES, 2 * LANES), f32),
        ],
        compiler_params=pltpu.CompilerParams(vmem_limit_bytes=VMEM_LIMIT),
        cost_estimate=pl.CostEstimate(flops=COST_A, bytes_accessed=1 << 20, transcendentals=0),
        name="prepare",
    )(near, own, far, end)
    band = pltpu.VMEM((BROWS, LANES), f32)
    out = pl.pallas_call(
        functools.partial(profile, geo),
        out_shape=jax.ShapeDtypeStruct((share_rows, LANES), f32),
        in_specs=[vmem] * 9,
        out_specs=vmem,
        scratch_shapes=[
            pltpu.VMEM((2 * groups, -(-(share_rows + 3) // SUB) * SUB, LANES), f32),
            band,
            band,
            band,
            band,
            band,
            pltpu.VMEM((M * SUB, LANES), f32),
        ],
        compiler_params=pltpu.CompilerParams(vmem_limit_bytes=VMEM_LIMIT),
        cost_estimate=pl.CostEstimate(flops=1 << 24, bytes_accessed=1 << 20, transcendentals=0),
        name="profile",
    )(rows(mine), rows(other), *tables)
    return out.reshape(-1)


def solution(mesh):
    in_specs = (P("tm"), P(), P("diag"), P())
    out_specs = P(("tm", "diag"))
    return jax.shard_map(
        on_device, mesh=mesh, in_specs=in_specs, out_specs=out_specs, check_vma=False
    )
```

time: 16.8 us -> 15.7 us (0.935)
  Pallas kernels: 6.68 us -> 4.37 us
  waiting for transfers between devices: 0.2 us -> 1.38 us
    pallas_call x1, Pallas kernels: 1.68 us -> 0.5 us  [on_device(): pl.pallas_call(functools.partial(prepare, geo), out_shape=[table] * 7, in...]
    ppermute x4, waiting for transfers between devices: 0.2 us -> 1.38 us  [swapped(): lax.ppermute(shard, axis, [(i, partner(i) % size) for i in range(size)])]
    pallas_call x1, Pallas kernels: 4.14 us -> 3.02 us  [on_device(): pl.pallas_call(functools.partial(profile, geo), out_shape=jax.ShapeDtypeS...]
  transfers between devices with their start and end apart: 4 -> 4, of which waited for: 1 -> 1; matrix products, arithmetic and copies ran while one was open for 0% -> 0% of each run, Pallas kernels for 15% -> 9%
where the time goes in v4:
time: 15.7 us; the launch traced here: 15.5 us
  starting transfers between devices  8.39 us (53%)
  Pallas kernels  4.37 us (28%)
  waiting for transfers between devices  1.38 us (9%)
  between operations  1.35 us (9%)
    ppermute x4, starting transfers between devices, swapped(): lax.ppermute(shard, axis, [(i, partner(i) % size) for i in range(size)])  8.39 us
    pallas_call x1, Pallas kernels, on_device(): pl.pallas_call(functools.partial(profile, geo), out_shape=jax.ShapeDtypeS...  3.02 us
    ppermute x4, waiting for transfers between devices, swapped(): lax.ppermute(shard, axis, [(i, partner(i) % size) for i in range(size)])  1.38 us
    pallas_call x1, Pallas kernels, on_device(): pl.pallas_call(stage, out_shape=[jax.ShapeDtypeStruct((segrows, LANES), f...  0.86 us
    pallas_call x1, Pallas kernels, on_device(): pl.pallas_call(functools.partial(prepare, geo), out_shape=[table] * 7, in...  0.5 us
  transfers between devices with their start and end apart: 4, of which 1 were waited for; matrix products, arithmetic and copies ran while one was open for 0% of the time, Pallas kernels for 9%

profile of v4, /device:TPU:0, one launch (start us, length us, event | category | flops | bytes accessed | tf_op | source)
XLA Modules:
  0.0 15.5 jit_solution(1875556796697782309)
XLA Ops:
  0.7 3.1 %collective-permute-start = (s32[128]{0:T(128)S(1)}, s32[128]{0:T(128)S(1)}, u32[]{:S(2)}, u32[]{:S(2)}) collective-permute-start(s32[128]{0:T(128)S(1)} %compare_select_fusion.1), channel_id=1, source_target_pairs={{0,1},{1,0},{2,3},{3,2},{4,5},{5,4},{6,7},{7,6},{8,9},{9,8},{10,11... | collective-permute-start | bytes 1544 | tf_op jit(solution)/shard_map/ppermute | solution.py:26
  3.8 0.9 %stage.1 = (f32[128,128]{1,0:T(8,128)S(1)}, f32[2,128]{1,0:T(2,128)S(1)}) custom-call(f32[128,128]{1,0:T(8,128)} %bitcast.12, f32[2,128]{1,0:T(2,128)} %bitcast.13), custom_call_target="tpu_custom_call" | custom-call | flops 2097152 | bytes 131072 | tf_op jit(solution)/shard_map/stage/pallas_call | solution.py:266
  4.6 0.1 collective-permute-start.2
  4.7 2.5 %collective-permute-start.3 = (f32[128,128]{1,0:T(8,128)S(1)}, f32[128,128]{1,0:T(8,128)S(1)}, u32[]{:S(2)}, u32[]{:S(2)}) collective-permute-start(f32[128,128]{1,0:T(8,128)S(1)} %get-tuple-element.14.own_ref), channel_id=1, source_target_pairs={{0,28},{4,8},{8,4},{12,16},{16,12},{20,24},{24,20},{28,0},{1,29},{... | collective-permute-start | bytes 196616 | tf_op jit(solution)/shard_map/ppermute | solution.py:26
  7.9 0.0 collective-permute-done
  8.0 2.7 %collective-permute-start.1 = (s32[128]{0:T(128)S(1)}, s32[128]{0:T(128)S(1)}, u32[]{:S(2)}, u32[]{:S(2)}) collective-permute-start(s32[128]{0:T(128)S(1)} %get-tuple-element.24), channel_id=1, source_target_pairs={{0,2},{1,3},{2,0},{3,1},{4,6},{5,7},{6,4},{7,5},{8,10},{9,11},{10,... | collective-permute-start | bytes 1544 | tf_op jit(solution)/shard_map/ppermute | solution.py:26
  10.6 0.0 collective-permute-done.2.near_ref
  10.6 0.0 collective-permute-done.3.far_ref
  10.6 0.5 %prepare.1 = (f32[256,128]{1,0:T(8,128)S(1)}, f32[256,128]{1,0:T(8,128)S(1)}, f32[256,128]{1,0:T(8,128)S(1)}, f32[256,128]{1,0:T(8,128)S(1)}, f32[256,128]{1,0:T...) custom-call(f32[128,128]{1,0:T(8,128)S(1)} %collective-permute-done.2.near_ref, ...), custom_call_target="tpu_custom_call" | custom-call | flops 8388608 | bytes 1048576 | tf_op jit(solution)/shard_map/prepare/pallas_call | solution.py:282
  11.1 1.4 %collective-permute-done.1 = s32[128]{0:T(128)S(1)} collective-permute-done((s32[128]{0:T(128)S(1)}, s32[128]{0:T(128)S(1)}, u32[]{:S(2)}, u32[]{:S(2)}) %collective-permute-start.1) | collective-permute-done | bytes 544 | tf_op jit(solution)/shard_map/ppermute | solution.py:26
  12.5 3.0 %profile.1 = f32[32,128]{1,0:T(8,128)} custom-call(s32[1,128]{1,0:T(1,128)S(1)} %get-tuple-element.23.mine_ref, s32[1,128]{1,0:T(1,128)S(1)} %bitcast.11, f32[256,128]{1,0:T(8,128)S(1)} %get-tuple-element.16.points, f32[256,128]{1,0:T(8,128)S(1)} %get-tuple-element.17.fall, f32[256,128]{1,0:T(8,128)S(1)} %get-tuple-element.18.rise, ...), custom_call_target="tpu_custom_call" | custom-call | flops 16777216 | bytes 1048576 | tf_op jit(solution)/shard_map/profile/pallas_call | solution.py:296
  (2 shorter events, 0.0 us)
Async XLA Ops:
  0.7 7.3 %collective-permute-start = (s32[128]{0:T(128)S(1)}, s32[128]{0:T(128)S(1)}, u32[]{:S(2)}, u32[]{:S(2)}) collective-permute-start(s32[128]{0:T(128)S(1)} %compare_select_fusion.1), channel_id=1, source_target_pairs={{0,1},{1,0},{2,3},{3,2},{4,5},{5,4},{6,7},{7,6},{8,9},{9,8},{10,11... | collective-permute-start | bytes 1544 | tf_op jit(solution)/shard_map/ppermute | solution.py:26
  4.6 6.0 %collective-permute-start.2 = (f32[128,128]{1,0:T(8,128)S(1)}, f32[128,128]{1,0:T(8,128)S(1)}, u32[]{:S(2)}, u32[]{:S(2)}) collective-permute-start(f32[128,128]{1,0:T(8,128)S(1)} %get-tuple-element.14.own_ref), channel_id=1, source_target_pairs={{0,4},{4,0},{8,12},{12,8},{16,20},{20,16},{24,28},{28,24},{1,5},{5... | collective-permute-start | bytes 196616 | tf_op jit(solution)/shard_map/ppermute | solution.py:26
  4.7 5.9 %collective-permute-start.3 = (f32[128,128]{1,0:T(8,128)S(1)}, f32[128,128]{1,0:T(8,128)S(1)}, u32[]{:S(2)}, u32[]{:S(2)}) collective-permute-start(f32[128,128]{1,0:T(8,128)S(1)} %get-tuple-element.14.own_ref), channel_id=1, source_target_pairs={{0,28},{4,8},{8,4},{12,16},{16,12},{20,24},{24,20},{28,0},{1,29},{... | collective-permute-start | bytes 196616 | tf_op jit(solution)/shard_map/ppermute | solution.py:26
  8.0 4.5 %collective-permute-start.1 = (s32[128]{0:T(128)S(1)}, s32[128]{0:T(128)S(1)}, u32[]{:S(2)}, u32[]{:S(2)}) collective-permute-start(s32[128]{0:T(128)S(1)} %get-tuple-element.24), channel_id=1, source_target_pairs={{0,2},{1,3},{2,0},{3,1},{4,6},{5,7},{6,4},{7,5},{8,10},{9,11},{10,... | collective-permute-start | bytes 1544 | tf_op jit(solution)/shard_map/ppermute | solution.py:26

commit v5 on v4

--- a/solution.py
+++ b/solution.py
@@ -12,10 +12,13 @@
 FILL = 1e30
 LANES = 128
 SUB = 8
-STEP = KB // SUB
-BROWS = M + KB
+HALF = KB // 2
+STEP = HALF // SUB
+BROWS = M + HALF
+SPAN = M + 4
 BIG = 1e30
-UNROLL = 8
+UNROLL = 64
+TOTALS = 4
 VMEM_LIMIT = 16 << 20
 COST_A = 1 << 23
 COST_STAGE = 1 << 21
@@ -142,27 +145,25 @@
     own_rise[...] = own_rows(rise)
 
 
-def profile(geo, mine_ref, other_ref, points, fall, rise, spreads, own_points, own_fall, own_rise,
-            out_ref, moved, xband, fband, rband, sband, pband, best):
+def sweep(geo, offsets, excl, tables, scratch, before, best):
+    points, fall, rise, spreads, own_points, own_fall, own_rise = tables
+    moved, xband, fband, rband, sband, pband = scratch
     segrows, share_rows, back, groups, places = geo
     place = lax.axis_index("tm")
     diag = lax.axis_index("diag")
-    offsets = mine_ref[...] + other_ref[...]
-    excl = mine_ref[0, LANES - 1]
     chunks = share_rows // 2
 
     lane = lax.broadcasted_iota(jnp.int32, (1, LANES), 1)
     sub = lax.broadcasted_iota(jnp.int32, (SUB, LANES), 0)
-    lags, bases = [], []
-    for way in range(2):
-        for g in range(groups):
-            off = offsets[0, g]
-            lags.append(off if way == 0 else -(off + (KB - 1)))
+    lags = []
+    for off in offsets:
+        for lag in (off, -(off + (KB - 1))):
+            lags += [lag, lag + HALF]
     first_lag = jnp.zeros((1, LANES), jnp.int32)
     for j, lag in enumerate(lags):
         first_lag = jnp.where(lane >= chunks * j, lag, first_lag)
     rows = moved.shape[1]
-    for ref, out in ((points, xband), (spreads, sband), (fall, fband), (rise, rband)):
+    def fill(ref, out):
         parts = [[] for _ in range(3)]
         for j, lag in enumerate(lags):
             base = back * LANES + lag
@@ -180,38 +181,38 @@
                     )
                 )
         for q in range(3):
+            held = min(LANES, BROWS - q * LANES)
             turned = jnp.concatenate(parts[q], axis=0).T
-            out[q * LANES : min((q + 1) * LANES, BROWS), :] = turned[0 : min(LANES, BROWS - q * LANES)]
+            out[q * LANES : q * LANES + held, :] = turned[0:held]
+
+    def band(ref, start):
+        return ref[pl.ds(start, SUB, stride=STEP), :]
+
+    def row(ref, i):
+        return ref[pl.ds(i, SUB, stride=0), :]
+
+    fill(points, xband)
+    totals = [None] * (TOTALS * STEP)
+    for i in range(M):
+        xi = row(own_points, i)
+        for s in range(STEP):
+            c = s + STEP * (i % TOTALS)
+            term = xi * band(xband, i + s)
+            totals[c] = term if totals[c] is None else totals[c] + term
+    start = []
+    for s in range(STEP):
+        parts = list(totals[s::STEP])
+        while len(parts) > 1:
+            parts = [a + b for a, b in zip(parts[0::2], parts[1::2])]
+        start.append(jnp.where(jnp.abs(first_lag + STEP * sub + s) < excl, -BIG, parts[0]))
+    fill(spreads, sband)
+    fill(fall, fband)
+    fill(rise, rband)
     limit = places * segrows * LANES
     own_start = (place * segrows + share_rows * diag) * LANES
     position = own_start + (lane & (chunks - 1)) * M + first_lag
     position = position + lax.broadcasted_iota(jnp.int32, (BROWS, LANES), 0)
     pband[...] = jnp.where((position >= 0) & (position < limit), BIG, -BIG)
-
-    def band(ref, start):
-        return ref[pl.ds(start, SUB, stride=STEP), :]
-
-    def row(ref, i):
-        return ref[pl.ds(i, SUB, stride=0), :]
-
-    def first(step, totals):
-        totals = list(totals)
-        for u in range(UNROLL):
-            i = step * UNROLL + u
-            xi = row(own_points, i)
-            for s in range(STEP):
-                c = s + STEP * (u % 2)
-                totals[c] = totals[c] + xi * band(xband, i + s)
-        return tuple(totals)
-
-    zero = jnp.zeros((SUB, LANES), jnp.float32)
-    totals = lax.fori_loop(0, M // UNROLL, first, (zero,) * (2 * STEP))
-    start = tuple(
-        jnp.where(
-            jnp.abs(first_lag + STEP * sub + s) < excl, -BIG, totals[s] + totals[s + STEP]
-        )
-        for s in range(STEP)
-    )
 
     def advance(step, covs):
         covs = list(covs)
@@ -219,23 +220,43 @@
             i = step * UNROLL + u
             fi = row(own_fall, i)
             ri = row(own_rise, i)
-            top = None
+            top = None if before is None else before[pl.ds(i, SUB, stride=SPAN), :]
             for s in range(STEP):
                 value = jnp.minimum(covs[s] * band(sband, i + s), band(pband, i + s))
                 top = value if top is None else jnp.maximum(top, value)
                 covs[s] = covs[s] + (fi * band(rband, i + s) + ri * band(fband, i + s))
-            best[pl.ds(pl.multiple_of(i * SUB, SUB), SUB), :] = top
+            best[pl.ds(i, SUB, stride=SPAN), :] = top
         return tuple(covs)
 
-    lax.fori_loop(0, M // UNROLL, advance, start)
+    lax.fori_loop(0, M // UNROLL, advance, tuple(start))
+
+
+def picked(slots, groups):
+    half = groups // 2
+    return [slots[0, e] + slots[0, half + e] for e in range(half)]
+
+
+def early(geo, mine_ref, *refs):
+    tables, best, scratch = refs[:7], refs[7], refs[8:]
+    slots = mine_ref[...]
+    sweep(geo, picked(slots, geo[3]), slots[0, LANES - 1], tables, scratch, None, best)
+
+
+def late(geo, mine_ref, other_ref, before, *refs):
+    tables, out_ref, best, scratch = refs[:7], refs[7], refs[8], refs[9:]
+    segrows, share_rows, back, groups, places = geo
+    chunks = share_rows // 2
+    excl = mine_ref[0, LANES - 1]
+    sweep(geo, picked(other_ref[...], groups), excl, tables, scratch, before, best)
+    spreads = tables[3]
 
     for half in range(2):
         blocks = []
         for block in range(LANES // SUB):
             top = None
             for h in range(SUB):
-                at = (half * LANES + block * SUB) * SUB + h
-                part = best[pl.ds(at, SUB, stride=SUB), :]
+                at = h * SPAN + half * LANES + block * SUB
+                part = best[at : at + SUB, :]
                 top = part if top is None else jnp.maximum(top, part)
             blocks.append(top)
         turned = jnp.concatenate(blocks, axis=0).T
@@ -293,24 +314,29 @@
         name="prepare",
     )(near, own, far, end)
     band = pltpu.VMEM((BROWS, LANES), f32)
+    moved = pltpu.VMEM((2 * groups, -(-(share_rows + 3) // SUB) * SUB, LANES), f32)
+    scratch = [moved, band, band, band, band, band]
+    params = pltpu.CompilerParams(vmem_limit_bytes=VMEM_LIMIT)
+    maxima = pl.pallas_call(
+        functools.partial(early, geo),
+        out_shape=jax.ShapeDtypeStruct((SUB * SPAN, LANES), f32),
+        in_specs=[vmem] * 8,
+        out_specs=vmem,
+        scratch_shapes=scratch,
+        compiler_params=params,
+        cost_estimate=pl.CostEstimate(flops=COST_A, bytes_accessed=1 << 20, transcendentals=0),
+        name="early",
+    )(rows(mine), *tables)
     out = pl.pallas_call(
-        functools.partial(profile, geo),
+        functools.partial(late, geo),
         out_shape=jax.ShapeDtypeStruct((share_rows, LANES), f32),
-        in_specs=[vmem] * 9,
+        in_specs=[vmem] * 10,
         out_specs=vmem,
-        scratch_shapes=[
-            pltpu.VMEM((2 * groups, -(-(share_rows + 3) // SUB) * SUB, LANES), f32),
-            band,
-            band,
-            band,
-            band,
-            band,
-            pltpu.VMEM((M * SUB, LANES), f32),
-        ],
-        compiler_params=pltpu.CompilerParams(vmem_limit_bytes=VMEM_LIMIT),
+        scratch_shapes=[pltpu.VMEM((SUB * SPAN, LANES), f32)] + scratch,
+        compiler_params=params,
         cost_estimate=pl.CostEstimate(flops=1 << 24, bytes_accessed=1 << 20, transcendentals=0),
-        name="profile",
-    )(rows(mine), rows(other), *tables)
+        name="late",
+    )(rows(mine), rows(other), maxima, *tables)
     return out.reshape(-1)
 
 

time: 15.7 us -> 13.6 us (0.87)
  waiting for transfers between devices: 1.38 us -> 0.26 us
  starting transfers between devices: 8.39 us -> 7.45 us
    ppermute x4, waiting for transfers between devices: 1.38 us -> 0.26 us  [swapped(): lax.ppermute(shard, axis, [(i, partner(i) % size) for i in range(size)])]
    ppermute x4, starting transfers between devices: 8.39 us -> 7.45 us  [swapped(): lax.ppermute(shard, axis, [(i, partner(i) % size) for i in range(size)])]
    pallas_call x1 -> x2, Pallas kernels: 3.02 us -> 3.04 us  [the longest x1 1.91 us: on_device(): pl.pallas_call(functools.partial(late, geo), out_shape=jax.ShapeDtypeStru...]
  transfers between devices with their start and end apart: 4 -> 4, of which waited for: 1 -> 1; matrix products, arithmetic and copies ran while one was open for 0% -> 0% of each run, Pallas kernels for 9% -> 18%
where the time goes in v5:
time: 13.6 us; the launch traced here: 13.5 us
  starting transfers between devices  7.45 us (55%)
  Pallas kernels  4.39 us (32%)
  between operations  1.36 us (10%)
  waiting for transfers between devices  0.26 us (2%)
    ppermute x4, starting transfers between devices, swapped(): lax.ppermute(shard, axis, [(i, partner(i) % size) for i in range(size)])  7.45 us
    pallas_call x1, Pallas kernels, on_device(): pl.pallas_call(functools.partial(late, geo), out_shape=jax.ShapeDtypeStru...  1.91 us
    pallas_call x1, Pallas kernels, on_device(): pl.pallas_call(functools.partial(early, geo), out_shape=jax.ShapeDtypeStr...  1.14 us
    pallas_call x1, Pallas kernels, on_device(): pl.pallas_call(stage, out_shape=[jax.ShapeDtypeStruct((segrows, LANES), f...  0.86 us
    pallas_call x1, Pallas kernels, on_device(): pl.pallas_call(functools.partial(prepare, geo), out_shape=[table] * 7, in...  0.49 us
  transfers between devices with their start and end apart: 4, of which 1 were waited for; matrix products, arithmetic and copies ran while one was open for 0% of the time, Pallas kernels for 18%

profile of v5, /device:TPU:0, one launch (start us, length us, event | category | flops | bytes accessed | tf_op | source)
XLA Modules:
  0.0 13.5 jit_solution(10006401347430270011)
XLA Ops:
  0.7 3.1 %collective-permute-start = (s32[128]{0:T(128)S(1)}, s32[128]{0:T(128)S(1)}, u32[]{:S(2)}, u32[]{:S(2)}) collective-permute-start(s32[128]{0:T(128)S(1)} %compare_select_fusion.1), channel_id=1, source_target_pairs={{0,1},{1,0},{2,3},{3,2},{4,5},{5,4},{6,7},{7,6},{8,9},{9,8},{10,11... | collective-permute-start | bytes 1544 | tf_op jit(solution)/shard_map/ppermute | solution.py:29
  3.8 0.9 %stage.1 = (f32[128,128]{1,0:T(8,128)S(1)}, f32[2,128]{1,0:T(2,128)S(1)}) custom-call(f32[128,128]{1,0:T(8,128)} %bitcast.12, f32[2,128]{1,0:T(2,128)} %bitcast.13), custom_call_target="tpu_custom_call" | custom-call | flops 2097152 | bytes 131072 | tf_op jit(solution)/shard_map/stage/pallas_call | solution.py:287
  4.6 1.7 %collective-permute-start.3 = (f32[128,128]{1,0:T(8,128)S(1)}, f32[128,128]{1,0:T(8,128)S(1)}, u32[]{:S(2)}, u32[]{:S(2)}) collective-permute-start(f32[128,128]{1,0:T(8,128)S(1)} %get-tuple-element.14.own_ref), channel_id=1, source_target_pairs={{0,28},{4,8},{8,4},{12,16},{16,12},{20,24},{24,20},{28,0},{1,29},{... | collective-permute-start | bytes 196616 | tf_op jit(solution)/shard_map/ppermute | solution.py:29
  6.3 0.0 collective-permute-start.2
  7.0 0.0 collective-permute-done
  7.0 2.7 %collective-permute-start.1 = (s32[128]{0:T(128)S(1)}, s32[128]{0:T(128)S(1)}, u32[]{:S(2)}, u32[]{:S(2)}) collective-permute-start(s32[128]{0:T(128)S(1)} %get-tuple-element.24), channel_id=1, source_target_pairs={{0,2},{1,3},{2,0},{3,1},{4,6},{5,7},{6,4},{7,5},{8,10},{9,11},{10,... | collective-permute-start | bytes 1544 | tf_op jit(solution)/shard_map/ppermute | solution.py:29
  9.7 0.2 %collective-permute-done.3.far_ref = f32[128,128]{1,0:T(8,128)S(1)} collective-permute-done((f32[128,128]{1,0:T(8,128)S(1)}, f32[128,128]{1,0:T(8,128)S(1)}, u32[]{:S(2)}, u32[]{:S(2)}) %collective-permute-start.3) | collective-permute-done | bytes 65568 | tf_op jit(solution)/shard_map/ppermute | solution.py:29
  9.9 0.0 collective-permute-done.2.near_ref
  9.9 0.5 %prepare.1 = (f32[256,128]{1,0:T(8,128)S(1)}, f32[256,128]{1,0:T(8,128)S(1)}, f32[256,128]{1,0:T(8,128)S(1)}, f32[256,128]{1,0:T(8,128)S(1)}, f32[256,128]{1,0:T...) custom-call(f32[128,128]{1,0:T(8,128)S(1)} %collective-permute-done.2.near_ref, ...), custom_call_target="tpu_custom_call" | custom-call | flops 8388608 | bytes 1048576 | tf_op jit(solution)/shard_map/prepare/pallas_call | solution.py:303
  10.4 1.1 %early.1.before = f32[2080,128]{1,0:T(8,128)S(1)} custom-call(s32[1,128]{1,0:T(1,128)S(1)} %get-tuple-element.23.mine_ref, f32[256,128]{1,0:T(8,128)S(1)} %get-tuple-element.16.refs_0_, f32[256,128]{1,0:T(8,128)S(1)} %get-tuple-element.17.refs_1_, f32[256,128]{1,0:T(8,128)S(1)} %get-tuple-element.18.refs_2_, f32[256,128]{1,0:T(8,128)S(1)} %get-tuple-element.19.refs_3_, ...), custom_call_target="tpu_custom_call" | custom-call | flops 8388608 | bytes 1048576 | tf_op jit(solution)/shard_map/early/pallas_call | solution.py:320
  11.5 0.0 collective-permute-done.1
  11.6 1.9 %late.1 = f32[32,128]{1,0:T(8,128)} custom-call(s32[1,128]{1,0:T(1,128)S(1)} %get-tuple-element.23.mine_ref, s32[1,128]{1,0:T(1,128)S(1)} %bitcast.11, f32[2080,128]{1,0:T(8,128)S(1)} %early.1.before, f32[256,128]{1,0:T(8,128)S(1)} %get-tuple-element.16.refs_0_, f32[256,128]{1,0:T(8,128)S(1)} %get-tuple-element.17.refs_1_, ...), custom_call_target="tpu_custom_call" | custom-call | flops 16777216 | bytes 1048576 | tf_op jit(solution)/shard_map/late/pallas_call | solution.py:330
  (2 shorter events, 0.0 us)
Async XLA Ops:
  0.7 6.3 %collective-permute-start = (s32[128]{0:T(128)S(1)}, s32[128]{0:T(128)S(1)}, u32[]{:S(2)}, u32[]{:S(2)}) collective-permute-start(s32[128]{0:T(128)S(1)} %compare_select_fusion.1), channel_id=1, source_target_pairs={{0,1},{1,0},{2,3},{3,2},{4,5},{5,4},{6,7},{7,6},{8,9},{9,8},{10,11... | collective-permute-start | bytes 1544 | tf_op jit(solution)/shard_map/ppermute | solution.py:29
  4.6 5.3 %collective-permute-start.3 = (f32[128,128]{1,0:T(8,128)S(1)}, f32[128,128]{1,0:T(8,128)S(1)}, u32[]{:S(2)}, u32[]{:S(2)}) collective-permute-start(f32[128,128]{1,0:T(8,128)S(1)} %get-tuple-element.14.own_ref), channel_id=1, source_target_pairs={{0,28},{4,8},{8,4},{12,16},{16,12},{20,24},{24,20},{28,0},{1,29},{... | collective-permute-start | bytes 196616 | tf_op jit(solution)/shard_map/ppermute | solution.py:29
  6.3 3.6 %collective-permute-start.2 = (f32[128,128]{1,0:T(8,128)S(1)}, f32[128,128]{1,0:T(8,128)S(1)}, u32[]{:S(2)}, u32[]{:S(2)}) collective-permute-start(f32[128,128]{1,0:T(8,128)S(1)} %get-tuple-element.14.own_ref), channel_id=1, source_target_pairs={{0,4},{4,0},{8,12},{12,8},{16,20},{20,16},{24,28},{28,24},{1,5},{5... | collective-permute-start | bytes 196616 | tf_op jit(solution)/shard_map/ppermute | solution.py:29
  7.0 4.6 %collective-permute-start.1 = (s32[128]{0:T(128)S(1)}, s32[128]{0:T(128)S(1)}, u32[]{:S(2)}, u32[]{:S(2)}) collective-permute-start(s32[128]{0:T(128)S(1)} %get-tuple-element.24), channel_id=1, source_target_pairs={{0,2},{1,3},{2,0},{3,1},{4,6},{5,7},{6,4},{7,5},{8,10},{9,11},{10,... | collective-permute-start | bytes 1544 | tf_op jit(solution)/shard_map/ppermute | solution.py:29

commit v6 on v5

--- a/solution.py
+++ b/solution.py
@@ -7,10 +7,12 @@
 from jax.experimental.pallas import tpu as pltpu
 from jax.sharding import PartitionSpec as P
 
+
 M = 256
 KB = 32
 FILL = 1e30
 LANES = 128
+LANE_BITS = 7
 SUB = 8
 HALF = KB // 2
 STEP = HALF // SUB
@@ -21,7 +23,7 @@
 TOTALS = 4
 VMEM_LIMIT = 16 << 20
 COST_A = 1 << 23
-COST_STAGE = 1 << 21
+COST_LOW = 1 << 30
 
 
 def swapped(shard, axis, partner):
@@ -58,20 +60,17 @@
     return out
 
 
-def stage(series_ref, tail_ref, series_out, tail_out, sems):
-    copies = [
-        pltpu.make_async_copy(series_ref, series_out, sems.at[0]),
-        pltpu.make_async_copy(tail_ref, tail_out, sems.at[1]),
-    ]
-    for copy in copies:
-        copy.start()
-    for copy in copies:
-        copy.wait()
-
-
-def prepare(geo, near_ref, own_ref, far_ref, tail_ref,
+def triangles(ones):
+    rid = lax.broadcasted_iota(jnp.int32, (LANES, 2 * LANES), 0)
+    cid = lax.broadcasted_iota(jnp.int32, (LANES, 2 * LANES), 1)
+    ones[...] = jnp.where(
+        cid < LANES, (rid >= cid).astype(jnp.float32), (rid < cid - LANES).astype(jnp.float32)
+    ).astype(jnp.bfloat16)
+
+
+def prepare(geo, near_ref, own_ref, far_ref, tail_ref, ones_ref,
             points, fall, rise, spreads, own_points, own_fall, own_rise, ext, sums):
-    segrows, share_rows, back, groups, places = geo
+    segrows, share_rows, back, _, places = geo
     place = lax.axis_index("tm")
     diag = lax.axis_index("diag")
 
@@ -102,11 +101,7 @@
     first_row = pl.multiple_of(segrows - back + share_rows * diag, SUB)
     points[...] = ext[pl.ds(first_row, 2 * LANES), :]
 
-    rid = lax.broadcasted_iota(jnp.int32, (LANES, 2 * LANES), 0)
-    cid = lax.broadcasted_iota(jnp.int32, (LANES, 2 * LANES), 1)
-    ones = jnp.where(
-        cid < LANES, (rid >= cid).astype(jnp.float32), (rid < cid - LANES).astype(jnp.float32)
-    ).astype(jnp.bfloat16)
+    ones = ones_ref[...]
     held = 2 * LANES - SUB
 
     def windows(values):
@@ -148,7 +143,7 @@
 def sweep(geo, offsets, excl, tables, scratch, before, best):
     points, fall, rise, spreads, own_points, own_fall, own_rise = tables
     moved, xband, fband, rband, sband, pband = scratch
-    segrows, share_rows, back, groups, places = geo
+    segrows, share_rows, back, _, places = geo
     place = lax.axis_index("tm")
     diag = lax.axis_index("diag")
     chunks = share_rows // 2
@@ -162,22 +157,23 @@
     first_lag = jnp.zeros((1, LANES), jnp.int32)
     for j, lag in enumerate(lags):
         first_lag = jnp.where(lane >= chunks * j, lag, first_lag)
-    rows = moved.shape[1]
-    def fill(ref, out):
+    rows = moved.shape[2]
+
+    def fill(n, ref, out):
         parts = [[] for _ in range(3)]
         for j, lag in enumerate(lags):
             base = back * LANES + lag
-            row = base // LANES
-            inner = base - row * LANES
-            turn = lax.rem(LANES - inner, LANES)
-            moved[j] = pltpu.roll(ref[pl.ds(row, rows), :], turn, 1)
+            row = lax.shift_right_logical(base, LANE_BITS)
+            inner = base & (LANES - 1)
+            turn = (LANES - inner) & (LANES - 1)
+            moved[n, j] = pltpu.roll(ref[pl.ds(row, rows), :], turn, 1)
             near = lane < LANES - inner
             for q in range(3):
                 parts[q].append(
                     jnp.where(
                         near,
-                        moved[j, pl.ds(q, chunks, stride=2), :],
-                        moved[j, pl.ds(q + 1, chunks, stride=2), :],
+                        moved[n, j, pl.ds(q, chunks, stride=2), :],
+                        moved[n, j, pl.ds(q + 1, chunks, stride=2), :],
                     )
                 )
         for q in range(3):
@@ -191,7 +187,7 @@
     def row(ref, i):
         return ref[pl.ds(i, SUB, stride=0), :]
 
-    fill(points, xband)
+    fill(0, points, xband)
     totals = [None] * (TOTALS * STEP)
     for i in range(M):
         xi = row(own_points, i)
@@ -205,9 +201,9 @@
         while len(parts) > 1:
             parts = [a + b for a, b in zip(parts[0::2], parts[1::2])]
         start.append(jnp.where(jnp.abs(first_lag + STEP * sub + s) < excl, -BIG, parts[0]))
-    fill(spreads, sband)
-    fill(fall, fband)
-    fill(rise, rband)
+    fill(1, spreads, sband)
+    fill(2, fall, fband)
+    fill(3, rise, rband)
     limit = places * segrows * LANES
     own_start = (place * segrows + share_rows * diag) * LANES
     position = own_start + (lane & (chunks - 1)) * M + first_lag
@@ -244,7 +240,7 @@
 
 def late(geo, mine_ref, other_ref, before, *refs):
     tables, out_ref, best, scratch = refs[:7], refs[7], refs[8], refs[9:]
-    segrows, share_rows, back, groups, places = geo
+    _, share_rows, back, groups, _ = geo
     chunks = share_rows // 2
     excl = mine_ref[0, LANES - 1]
     sweep(geo, picked(other_ref[...], groups), excl, tables, scratch, before, best)
@@ -280,30 +276,23 @@
     geo = (segrows, share_rows, back, groups, places)
     f32 = jnp.float32
     rows = lambda a: a.reshape(-1, LANES)
-    held = lambda a: pltpu.with_memory_space_constraint(a, pltpu.HBM)
     vmem = pl.BlockSpec(memory_space=pltpu.VMEM)
-    hbm = pl.BlockSpec(memory_space=pltpu.HBM)
     mine, other = group_offsets(diag_offsets, exclusion)
-    own, end = pl.pallas_call(
-        stage,
-        out_shape=[
-            jax.ShapeDtypeStruct((segrows, LANES), f32),
-            jax.ShapeDtypeStruct((M // LANES, LANES), f32),
-        ],
-        in_specs=[hbm] * 2,
-        out_specs=[vmem] * 2,
-        scratch_shapes=[pltpu.SemaphoreType.DMA((2,))],
+    ones = pl.pallas_call(
+        triangles,
+        out_shape=jax.ShapeDtypeStruct((LANES, 2 * LANES), jnp.bfloat16),
+        out_specs=vmem,
         compiler_params=pltpu.CompilerParams(vmem_limit_bytes=VMEM_LIMIT),
-        cost_estimate=pl.CostEstimate(flops=COST_STAGE, bytes_accessed=1 << 17, transcendentals=0),
-        name="stage",
-    )(held(rows(series)), held(rows(tail)))
-    far = swapped(own, "tm", lambda i: i + 1 if i % 2 else i - 1)
-    near = swapped(own, "tm", lambda i: i ^ 1)
+        cost_estimate=pl.CostEstimate(flops=COST_LOW, bytes_accessed=1 << 17, transcendentals=0),
+        name="triangles",
+    )()
+    far = swapped(series, "tm", lambda i: i + 1 if i % 2 else i - 1)
+    near = swapped(series, "tm", lambda i: i ^ 1)
     table = jax.ShapeDtypeStruct((2 * LANES, LANES), f32)
     tables = pl.pallas_call(
         functools.partial(prepare, geo),
         out_shape=[table] * 7,
-        in_specs=[vmem] * 4,
+        in_specs=[vmem] * 5,
         out_specs=[vmem] * 7,
         scratch_shapes=[
             pltpu.VMEM((max(3 * segrows, deepest + 2 * LANES), LANES), f32),
@@ -312,9 +301,9 @@
         compiler_params=pltpu.CompilerParams(vmem_limit_bytes=VMEM_LIMIT),
         cost_estimate=pl.CostEstimate(flops=COST_A, bytes_accessed=1 << 20, transcendentals=0),
         name="prepare",
-    )(near, own, far, end)
+    )(rows(near), rows(series), rows(far), rows(tail), ones)
     band = pltpu.VMEM((BROWS, LANES), f32)
-    moved = pltpu.VMEM((2 * groups, -(-(share_rows + 3) // SUB) * SUB, LANES), f32)
+    moved = pltpu.VMEM((4, 2 * groups, -(-(share_rows + 3) // SUB) * SUB, LANES), f32)
     scratch = [moved, band, band, band, band, band]
     params = pltpu.CompilerParams(vmem_limit_bytes=VMEM_LIMIT)
     maxima = pl.pallas_call(

time: 13.6 us -> 14.9 us (1.096)
  waiting for transfers between devices: 0.26 us -> 1.59 us
  Pallas kernels: 4.39 us -> 3.46 us
  starting transfers between devices: 7.45 us -> 8.27 us
    ppermute x4, waiting for transfers between devices: 0.26 us -> 1.59 us  [swapped(): lax.ppermute(shard, axis, [(i, partner(i) % size) for i in range(size)])]
    pallas_call x1, Pallas kernels: 0.86 us -> 0.02 us  [on_device(): pl.pallas_call(triangles, out_shape=jax.ShapeDtypeStruct((LANES, 2 * LANE...]
    ppermute x4, starting transfers between devices: 7.45 us -> 8.27 us  [swapped(): lax.ppermute(shard, axis, [(i, partner(i) % size) for i in range(size)])]
  transfers between devices with their start and end apart: 4 -> 4, of which waited for: 1 -> 2; matrix products, arithmetic and copies ran while one was open for 0% -> 0% of each run, Pallas kernels for 18% -> 11%
where the time goes in v6:
time: 14.9 us; the launch traced here: 14.7 us
  starting transfers between devices  8.27 us (56%)
  Pallas kernels  3.46 us (23%)
  waiting for transfers between devices  1.59 us (11%)
  between operations  1.35 us (9%)
    ppermute x4, starting transfers between devices, swapped(): lax.ppermute(shard, axis, [(i, partner(i) % size) for i in range(size)])  8.27 us
    pallas_call x1, Pallas kernels, on_device(): pl.pallas_call(functools.partial(late, geo), out_shape=jax.ShapeDtypeStru...  1.86 us
    ppermute x4, waiting for transfers between devices, swapped(): lax.ppermute(shard, axis, [(i, partner(i) % size) for i in range(size)])  1.59 us
    pallas_call x1, Pallas kernels, on_device(): pl.pallas_call(functools.partial(early, geo), out_shape=jax.ShapeDtypeStr...  1.1 us
    pallas_call x1, Pallas kernels, on_device(): pl.pallas_call(functools.partial(prepare, geo), out_shape=[table] * 7, in...  0.48 us
  transfers between devices with their start and end apart: 4, of which 2 were waited for; matrix products, arithmetic and copies ran while one was open for 0% of the time, Pallas kernels for 11%

profile of v6, /device:TPU:0, one launch (start us, length us, event | category | flops | bytes accessed | tf_op | source)
XLA Modules:
  0.0 14.7 jit_solution(14578884922208020450)
XLA Ops:
  0.0 0.5 %collective-permute-start.2 = (f32[16384]{0:T(1024)}, f32[16384]{0:T(1024)S(1)}, u32[]{:S(2)}, u32[]{:S(2)}) collective-permute-start(f32[16384]{0:T(1024)} %param.4), channel_id=1, source_target_pairs={{0,4},{4,0},{8,12},{12,8},{16,20},{20,16},{24,28},{28,24},{1,5},{5... | collective-permute-start | bytes 196616 | tf_op jit(solution)/shard_map/ppermute | solution.py:31
  0.5 3.5 %collective-permute-start.3 = (f32[16384]{0:T(1024)}, f32[16384]{0:T(1024)S(1)}, u32[]{:S(2)}, u32[]{:S(2)}) collective-permute-start(f32[16384]{0:T(1024)} %param.4), channel_id=1, source_target_pairs={{0,28},{4,8},{8,4},{12,16},{16,12},{20,24},{24,20},{28,0},{1,29},{... | collective-permute-start | bytes 196616 | tf_op jit(solution)/shard_map/ppermute | solution.py:31
  4.7 0.0 copy-start
  4.7 0.0 copy-start.1
  4.7 1.6 %collective-permute-start = (s32[128]{0:T(128)S(1)}, s32[128]{0:T(128)S(1)}, u32[]{:S(2)}, u32[]{:S(2)}) collective-permute-start(s32[128]{0:T(128)S(1)} %compare_select_fusion.1), channel_id=1, source_target_pairs={{0,1},{1,0},{2,3},{3,2},{4,5},{5,4},{6,7},{7,6},{8,9},{9,8},{10,11... | collective-permute-start | bytes 1544 | tf_op jit(solution)/shard_map/ppermute | solution.py:31
  7.0 1.3 %collective-permute-done = s32[128]{0:T(128)S(1)} collective-permute-done((s32[128]{0:T(128)S(1)}, s32[128]{0:T(128)S(1)}, u32[]{:S(2)}, u32[]{:S(2)}) %collective-permute-start) | collective-permute-done | bytes 544 | tf_op jit(solution)/shard_map/ppermute | solution.py:31
  8.4 2.6 %collective-permute-start.1 = (s32[128]{0:T(128)S(1)}, s32[128]{0:T(128)S(1)}, u32[]{:S(2)}, u32[]{:S(2)}) collective-permute-start(s32[128]{0:T(128)S(1)} %get-tuple-element.20), channel_id=1, source_target_pairs={{0,2},{1,3},{2,0},{3,1},{4,6},{5,7},{6,4},{7,5},{8,10},{9,11},{10,... | collective-permute-start | bytes 1544 | tf_op jit(solution)/shard_map/ppermute | solution.py:31
  11.0 0.0 collective-permute-done.2
  11.0 0.0 collective-permute-done.3
  11.0 0.0 copy-done
  11.0 0.0 copy-done.1
  11.0 0.5 %prepare.1 = (f32[256,128]{1,0:T(8,128)S(1)}, f32[256,128]{1,0:T(8,128)S(1)}, f32[256,128]{1,0:T(8,128)S(1)}, f32[256,128]{1,0:T(8,128)S(1)}, f32[256,128]{1,0:T...) custom-call(f32[128,128]{1,0:T(8,128)S(1)} %bitcast.14, f32[128,128]{1,0:T(8,128)S(1)} %bitcast.13, ...), custom_call_target="tpu_custom_call" | custom-call | flops 8388608 | bytes 1048576 | tf_op jit(solution)/shard_map/prepare/pallas_call | solution.py:292
  11.5 1.1 %early.1.before = f32[2080,128]{1,0:T(8,128)S(1)} custom-call(s32[1,128]{1,0:T(1,128)S(1)} %get-tuple-element.19.mine_ref, f32[256,128]{1,0:T(8,128)S(1)} %get-tuple-element.12.refs_0_, f32[256,128]{1,0:T(8,128)S(1)} %get-tuple-element.13.refs_1_, f32[256,128]{1,0:T(8,128)S(1)} %get-tuple-element.14.refs_2_, f32[256,128]{1,0:T(8,128)S(1)} %get-tuple-element.15.refs_3_, ...), custom_call_target="tpu_custom_call" | custom-call | flops 8388608 | bytes 1048576 | tf_op jit(solution)/shard_map/early/pallas_call | solution.py:309
  12.6 0.3 %collective-permute-done.1 = s32[128]{0:T(128)S(1)} collective-permute-done((s32[128]{0:T(128)S(1)}, s32[128]{0:T(128)S(1)}, u32[]{:S(2)}, u32[]{:S(2)}) %collective-permute-start.1) | collective-permute-done | bytes 544 | tf_op jit(solution)/shard_map/ppermute | solution.py:31
  12.8 1.9 %late.1 = f32[32,128]{1,0:T(8,128)} custom-call(s32[1,128]{1,0:T(1,128)S(1)} %get-tuple-element.19.mine_ref, s32[1,128]{1,0:T(1,128)S(1)} %bitcast.17, f32[2080,128]{1,0:T(8,128)S(1)} %early.1.before, f32[256,128]{1,0:T(8,128)S(1)} %get-tuple-element.12.refs_0_, f32[256,128]{1,0:T(8,128)S(1)} %get-tuple-element.13.refs_1_, ...), custom_call_target="tpu_custom_call" | custom-call | flops 16777216 | bytes 1048576 | tf_op jit(solution)/shard_map/late/pallas_call | solution.py:319
  (3 shorter events, 0.0 us)
Async XLA Ops:
  0.0 11.0 %collective-permute-start.2 = (f32[16384]{0:T(1024)}, f32[16384]{0:T(1024)S(1)}, u32[]{:S(2)}, u32[]{:S(2)}) collective-permute-start(f32[16384]{0:T(1024)} %param.4), channel_id=1, source_target_pairs={{0,4},{4,0},{8,12},{12,8},{16,20},{20,16},{24,28},{28,24},{1,5},{5... | collective-permute-start | bytes 196616 | tf_op jit(solution)/shard_map/ppermute | solution.py:31
  0.5 10.5 %collective-permute-start.3 = (f32[16384]{0:T(1024)}, f32[16384]{0:T(1024)S(1)}, u32[]{:S(2)}, u32[]{:S(2)}) collective-permute-start(f32[16384]{0:T(1024)} %param.4), channel_id=1, source_target_pairs={{0,28},{4,8},{8,4},{12,16},{16,12},{20,24},{24,20},{28,0},{1,29},{... | collective-permute-start | bytes 196616 | tf_op jit(solution)/shard_map/ppermute | solution.py:31
  4.7 6.3 %copy-start = (f32[16384]{0:T(1024)S(1)}, f32[16384]{0:T(1024)}, u32[]{:S(2)}) copy-start(f32[16384]{0:T(1024)} %param.4) | copy-start | bytes 196612
  4.7 6.3 %copy-start.1 = (f32[256]{0:T(256)S(1)}, f32[256]{0:T(256)}, u32[]{:S(2)}) copy-start(f32[256]{0:T(256)} %param.5) | copy-start | bytes 3076
  4.7 3.6 %collective-permute-start = (s32[128]{0:T(128)S(1)}, s32[128]{0:T(128)S(1)}, u32[]{:S(2)}, u32[]{:S(2)}) collective-permute-start(s32[128]{0:T(128)S(1)} %compare_select_fusion.1), channel_id=1, source_target_pairs={{0,1},{1,0},{2,3},{3,2},{4,5},{5,4},{6,7},{7,6},{8,9},{9,8},{10,11... | collective-permute-start | bytes 1544 | tf_op jit(solution)/shard_map/ppermute | solution.py:31
  8.4 4.5 %collective-permute-start.1 = (s32[128]{0:T(128)S(1)}, s32[128]{0:T(128)S(1)}, u32[]{:S(2)}, u32[]{:S(2)}) collective-permute-start(s32[128]{0:T(128)S(1)} %get-tuple-element.20), channel_id=1, source_target_pairs={{0,2},{1,3},{2,0},{3,1},{4,6},{5,7},{6,4},{7,5},{8,10},{9,11},{10,... | collective-permute-start | bytes 1544 | tf_op jit(solution)/shard_map/ppermute | solution.py:31

commit v7 on v6

--- a/solution.py
+++ b/solution.py
@@ -31,6 +31,21 @@
     return lax.ppermute(shard, axis, [(i, partner(i) % size) for i in range(size)])
 
 
+def across(shard):
+    places, groups = lax.axis_size("tm"), lax.axis_size("diag")
+
+    def partner(i, d):
+        other = i + 1 if i % 2 else i - 1
+        return (other, d) if 0 <= other < places else (i, d ^ 1)
+
+    pairs = []
+    for i in range(places):
+        for d in range(groups):
+            other, group = partner(i, d)
+            pairs.append((i * groups + d, other * groups + group))
+    return lax.ppermute(shard, ("tm", "diag"), pairs)
+
+
 def group_offsets(own, exclusion):
     size = lax.axis_size("diag")
     lanes = lax.iota(jnp.int32, LANES)
@@ -68,6 +83,22 @@
     ).astype(jnp.bfloat16)
 
 
+def relay(back, source, own, near, far):
+    rows = own.shape[0]
+    own[...] = source[...]
+    odd = lax.rem(lax.axis_index("tm"), 2) == 1
+
+    @pl.when(odd)
+    def _():
+        near[...] = source[0:back, :]
+        far[...] = source[rows - back : rows, :]
+
+    @pl.when(jnp.logical_not(odd))
+    def _():
+        near[...] = source[rows - back : rows, :]
+        far[...] = source[0:back, :]
+
+
 def prepare(geo, near_ref, own_ref, far_ref, tail_ref, ones_ref,
             points, fall, rise, spreads, own_points, own_fall, own_rise, ext, sums):
     segrows, share_rows, back, _, places = geo
@@ -78,26 +109,25 @@
     last = place == places - 1
     ext[segrows : 2 * segrows, :] = own_ref[...]
 
+    before, after = segrows - back, 2 * segrows + back
+
     @pl.when(odd)
     def _():
-        ext[0:segrows, :] = near_ref[...]
-        ext[2 * segrows : 3 * segrows, :] = far_ref[...]
+        ext[before:segrows, :] = near_ref[...]
+        ext[2 * segrows : after, :] = far_ref[...]
 
     @pl.when(jnp.logical_not(odd))
     def _():
-        ext[0:segrows, :] = far_ref[...]
-        ext[2 * segrows : 3 * segrows, :] = near_ref[...]
+        ext[before:segrows, :] = far_ref[...]
+        ext[2 * segrows : after, :] = near_ref[...]
 
     @pl.when(last)
     def _():
         tail_rows = M // LANES
         ext[2 * segrows : 2 * segrows + tail_rows, :] = tail_ref[...]
-        ext[2 * segrows + tail_rows : 3 * segrows, :] = jnp.zeros(
-            (segrows - tail_rows, LANES), jnp.float32
-        )
-
-    if ext.shape[0] > 3 * segrows:
-        ext[3 * segrows :, :] = jnp.zeros((ext.shape[0] - 3 * segrows, LANES), jnp.float32)
+        ext[2 * segrows + tail_rows : after, :] = jnp.zeros((back - tail_rows, LANES), jnp.float32)
+
+    ext[after:, :] = jnp.zeros((ext.shape[0] - after, LANES), jnp.float32)
     first_row = pl.multiple_of(segrows - back + share_rows * diag, SUB)
     points[...] = ext[pl.ds(first_row, 2 * LANES), :]
 
@@ -286,8 +316,21 @@
         cost_estimate=pl.CostEstimate(flops=COST_LOW, bytes_accessed=1 << 17, transcendentals=0),
         name="triangles",
     )()
-    far = swapped(series, "tm", lambda i: i + 1 if i % 2 else i - 1)
-    near = swapped(series, "tm", lambda i: i ^ 1)
+    own, low, high = pl.pallas_call(
+        functools.partial(relay, back),
+        out_shape=[
+            jax.ShapeDtypeStruct((segrows, LANES), f32),
+            jax.ShapeDtypeStruct((back, LANES), f32),
+            jax.ShapeDtypeStruct((back, LANES), f32),
+        ],
+        in_specs=[vmem],
+        out_specs=[vmem] * 3,
+        compiler_params=pltpu.CompilerParams(vmem_limit_bytes=VMEM_LIMIT),
+        cost_estimate=pl.CostEstimate(flops=1 << 10, bytes_accessed=1 << 17, transcendentals=0),
+        name="relay",
+    )(rows(series))
+    far = across(high)
+    near = swapped(low, "tm", lambda i: i ^ 1)
     table = jax.ShapeDtypeStruct((2 * LANES, LANES), f32)
     tables = pl.pallas_call(
         functools.partial(prepare, geo),
@@ -301,7 +344,7 @@
         compiler_params=pltpu.CompilerParams(vmem_limit_bytes=VMEM_LIMIT),
         cost_estimate=pl.CostEstimate(flops=COST_A, bytes_accessed=1 << 20, transcendentals=0),
         name="prepare",
-    )(rows(near), rows(series), rows(far), rows(tail), ones)
+    )(near, own, far, rows(tail), ones)
     band = pltpu.VMEM((BROWS, LANES), f32)
     moved = pltpu.VMEM((4, 2 * groups, -(-(share_rows + 3) // SUB) * SUB, LANES), f32)
     scratch = [moved, band, band, band, band, band]

time: 14.9 us -> 12.6 us (0.85)
  the two profiles are of different devices: /device:TPU:0 before, /device:TPU:1 now
where the time goes in v7:
time: 12.6 us; the launch traced here: 12.5 us
  starting transfers between devices  6.75 us (54%)
  Pallas kernels  3.48 us (28%)
  between operations  1.37 us (11%)
  local copies, waits for them, and re-layouts  0.84 us (7%)
    ppermute x3, starting transfers between devices, swapped(): lax.ppermute(shard, axis, [(i, partner(i) % size) for i in range(size)])  5.57 us
    pallas_call x1, Pallas kernels, on_device(): pl.pallas_call(functools.partial(late, geo), out_shape=jax.ShapeDtypeStru...  1.87 us
    ppermute x1, starting transfers between devices, across(): return lax.ppermute(shard, ('tm', 'diag'), pairs)  1.18 us
    pallas_call x1, Pallas kernels, on_device(): pl.pallas_call(functools.partial(early, geo), out_shape=jax.ShapeDtypeStr...  1.1 us
    unnamed x4, local copies, waits for them, and re-layouts  0.84 us
    pallas_call x1, Pallas kernels, on_device(): pl.pallas_call(functools.partial(prepare, geo), out_shape=[table] * 7, in...  0.48 us
  transfers between devices with their start and end apart: 4, of which 0 were waited for; matrix products, arithmetic and copies ran while one was open for 0% of the time, Pallas kernels for 13%

profile of v7, /device:TPU:1, one launch (start us, length us, event | category | flops | bytes accessed | tf_op | source)
XLA Modules:
  0.0 12.5 jit_solution(6569210878725859490)
XLA Ops:
  0.7 2.2 %collective-permute-start = (s32[128]{0:T(128)S(1)}, s32[128]{0:T(128)S(1)}, u32[]{:S(2)}, u32[]{:S(2)}) collective-permute-start(s32[128]{0:T(128)S(1)} %compare_select_fusion.1), channel_id=1, source_target_pairs={{0,1},{1,0},{2,3},{3,2},{4,5},{5,4},{6,7},{7,6},{8,9},{9,8},{10,11... | collective-permute-start | bytes 1544 | tf_op jit(solution)/shard_map/ppermute | solution.py:31
  2.8 0.0 copy-start
  2.8 0.8 %copy-done = f32[16384]{0:T(1024)S(1)} copy-done((f32[16384]{0:T(1024)S(1)}, f32[16384]{0:T(1024)}, u32[]{:S(2)}) %copy-start) | copy-done | bytes 65560
  3.7 1.0 %collective-permute-start.2 = (f32[96,128]{1,0:T(8,128)S(1)}, f32[96,128]{1,0:T(8,128)S(1)}, u32[]{:S(2)}, u32[]{:S(2)}) collective-permute-start(f32[96,128]{1,0:T(8,128)S(1)} %get-tuple-element.15), channel_id=1, source_target_pairs={{0,4},{4,0},{8,12},{12,8},{16,20},{20,16},{24,28},{28,24},{1,5},{5... | collective-permute-start | bytes 147464 | tf_op jit(solution)/shard_map/ppermute | solution.py:31
  4.7 0.0 copy-start.1
  4.7 1.2 %collective-permute-start.3 = (f32[96,128]{1,0:T(8,128)S(1)}, f32[96,128]{1,0:T(8,128)S(1)}, u32[]{:S(2)}, u32[]{:S(2)}) collective-permute-start(f32[96,128]{1,0:T(8,128)S(1)} %get-tuple-element.17), channel_id=1, source_target_pairs={{0,1},{1,0},{2,3},{3,2},{4,8},{5,9},{6,10},{7,11},{8,4},{9,5},{10,... | collective-permute-start | bytes 147464 | tf_op jit(solution)/shard_map/ppermute | solution.py:46
  6.6 0.0 collective-permute-done
  6.6 2.4 %collective-permute-start.1 = (s32[128]{0:T(128)S(1)}, s32[128]{0:T(128)S(1)}, u32[]{:S(2)}, u32[]{:S(2)}) collective-permute-start(s32[128]{0:T(128)S(1)} %get-tuple-element.26), channel_id=1, source_target_pairs={{0,2},{1,3},{2,0},{3,1},{4,6},{5,7},{6,4},{7,5},{8,10},{9,11},{10,... | collective-permute-start | bytes 1544 | tf_op jit(solution)/shard_map/ppermute | solution.py:31
  9.0 0.0 collective-permute-done.2.near_ref
  9.0 0.0 collective-permute-done.3.far_ref
  9.0 0.0 copy-done.1
  9.0 0.5 %prepare.1 = (f32[256,128]{1,0:T(8,128)S(1)}, f32[256,128]{1,0:T(8,128)S(1)}, f32[256,128]{1,0:T(8,128)S(1)}, f32[256,128]{1,0:T(8,128)S(1)}, f32[256,128]{1,0:T...) custom-call(f32[96,128]{1,0:T(8,128)S(1)} %collective-permute-done.2.near_ref, ...), custom_call_target="tpu_custom_call" | custom-call | flops 8388608 | bytes 1048576 | tf_op jit(solution)/shard_map/prepare/pallas_call | solution.py:335
  9.5 1.1 %early.1.before = f32[2080,128]{1,0:T(8,128)S(1)} custom-call(s32[1,128]{1,0:T(1,128)S(1)} %get-tuple-element.25.mine_ref, f32[256,128]{1,0:T(8,128)S(1)} %get-tuple-element.18.refs_0_, f32[256,128]{1,0:T(8,128)S(1)} %get-tuple-element.19.refs_1_, f32[256,128]{1,0:T(8,128)S(1)} %get-tuple-element.20.refs_2_, f32[256,128]{1,0:T(8,128)S(1)} %get-tuple-element.21.refs_3_, ...), custom_call_target="tpu_custom_call" | custom-call | flops 8388608 | bytes 1048576 | tf_op jit(solution)/shard_map/early/pallas_call | solution.py:352
  10.6 0.0 collective-permute-done.1
  10.6 1.9 %late.1 = f32[32,128]{1,0:T(8,128)} custom-call(s32[1,128]{1,0:T(1,128)S(1)} %get-tuple-element.25.mine_ref, s32[1,128]{1,0:T(1,128)S(1)} %bitcast.13, f32[2080,128]{1,0:T(8,128)S(1)} %early.1.before, f32[256,128]{1,0:T(8,128)S(1)} %get-tuple-element.18.refs_0_, f32[256,128]{1,0:T(8,128)S(1)} %get-tuple-element.19.refs_1_, ...), custom_call_target="tpu_custom_call" | custom-call | flops 16777216 | bytes 1048576 | tf_op jit(solution)/shard_map/late/pallas_call | solution.py:362
  (4 shorter events, 0.0 us)
Async XLA Ops:
  0.7 5.9 %collective-permute-start = (s32[128]{0:T(128)S(1)}, s32[128]{0:T(128)S(1)}, u32[]{:S(2)}, u32[]{:S(2)}) collective-permute-start(s32[128]{0:T(128)S(1)} %compare_select_fusion.1), channel_id=1, source_target_pairs={{0,1},{1,0},{2,3},{3,2},{4,5},{5,4},{6,7},{7,6},{8,9},{9,8},{10,11... | collective-permute-start | bytes 1544 | tf_op jit(solution)/shard_map/ppermute | solution.py:31
  2.8 0.8 %copy-start = (f32[16384]{0:T(1024)S(1)}, f32[16384]{0:T(1024)}, u32[]{:S(2)}) copy-start(f32[16384]{0:T(1024)} %param.4) | copy-start | bytes 196612
  3.7 5.3 %collective-permute-start.2 = (f32[96,128]{1,0:T(8,128)S(1)}, f32[96,128]{1,0:T(8,128)S(1)}, u32[]{:S(2)}, u32[]{:S(2)}) collective-permute-start(f32[96,128]{1,0:T(8,128)S(1)} %get-tuple-element.15), channel_id=1, source_target_pairs={{0,4},{4,0},{8,12},{12,8},{16,20},{20,16},{24,28},{28,24},{1,5},{5... | collective-permute-start | bytes 147464 | tf_op jit(solution)/shard_map/ppermute | solution.py:31
  4.7 4.3 %copy-start.1 = (f32[256]{0:T(256)S(1)}, f32[256]{0:T(256)}, u32[]{:S(2)}) copy-start(f32[256]{0:T(256)} %param.5) | copy-start | bytes 3076
  4.7 4.3 %collective-permute-start.3 = (f32[96,128]{1,0:T(8,128)S(1)}, f32[96,128]{1,0:T(8,128)S(1)}, u32[]{:S(2)}, u32[]{:S(2)}) collective-permute-start(f32[96,128]{1,0:T(8,128)S(1)} %get-tuple-element.17), channel_id=1, source_target_pairs={{0,1},{1,0},{2,3},{3,2},{4,8},{5,9},{6,10},{7,11},{8,4},{9,5},{10,... | collective-permute-start | bytes 147464 | tf_op jit(solution)/shard_map/ppermute | solution.py:46
  6.6 4.0 %collective-permute-start.1 = (s32[128]{0:T(128)S(1)}, s32[128]{0:T(128)S(1)}, u32[]{:S(2)}, u32[]{:S(2)}) collective-permute-start(s32[128]{0:T(128)S(1)} %get-tuple-element.26), channel_id=1, source_target_pairs={{0,2},{1,3},{2,0},{3,1},{4,6},{5,7},{6,4},{7,5},{8,10},{9,11},{10,... | collective-permute-start | bytes 1544 | tf_op jit(solution)/shard_map/ppermute | solution.py:31

commit v8 on v7

--- a/solution.py
+++ b/solution.py
@@ -180,10 +180,10 @@
 
     lane = lax.broadcasted_iota(jnp.int32, (1, LANES), 1)
     sub = lax.broadcasted_iota(jnp.int32, (SUB, LANES), 0)
-    lags = []
+    firsts = []
     for off in offsets:
-        for lag in (off, -(off + (KB - 1))):
-            lags += [lag, lag + HALF]
+        firsts += [off, -(off + (KB - 1))]
+    lags = firsts + [lag + HALF for lag in firsts]
     first_lag = jnp.zeros((1, LANES), jnp.int32)
     for j, lag in enumerate(lags):
         first_lag = jnp.where(lane >= chunks * j, lag, first_lag)
@@ -191,7 +191,7 @@
 
     def fill(n, ref, out):
         parts = [[] for _ in range(3)]
-        for j, lag in enumerate(lags):
+        for j, lag in enumerate(firsts):
             base = back * LANES + lag
             row = lax.shift_right_logical(base, LANE_BITS)
             inner = base & (LANES - 1)
@@ -206,10 +206,9 @@
                         moved[n, j, pl.ds(q + 1, chunks, stride=2), :],
                     )
                 )
-        for q in range(3):
-            held = min(LANES, BROWS - q * LANES)
-            turned = jnp.concatenate(parts[q], axis=0).T
-            out[q * LANES : q * LANES + held, :] = turned[0:held]
+        turned = [jnp.concatenate(parts[q] * 2, axis=0).T for q in range(3)]
+        whole = jnp.concatenate([turned[0], turned[1], turned[2][0 : 2 * HALF]], axis=0)
+        out[...] = jnp.where(lane < LANES // 2, whole[0:BROWS], whole[HALF : BROWS + HALF])
 
     def band(ref, start):
         return ref[pl.ds(start, SUB, stride=STEP), :]
@@ -346,7 +345,7 @@
         name="prepare",
     )(near, own, far, rows(tail), ones)
     band = pltpu.VMEM((BROWS, LANES), f32)
-    moved = pltpu.VMEM((4, 2 * groups, -(-(share_rows + 3) // SUB) * SUB, LANES), f32)
+    moved = pltpu.VMEM((4, groups, -(-(share_rows + 3) // SUB) * SUB, LANES), f32)
     scratch = [moved, band, band, band, band, band]
     params = pltpu.CompilerParams(vmem_limit_bytes=VMEM_LIMIT)
     maxima = pl.pallas_call(

time: 12.6 us -> 12.5 us (level)
  Pallas kernels: 3.48 us -> 3.35 us
where the time goes in v8:
time: 12.5 us; the launch traced here: 12.3 us
  starting transfers between devices  6.75 us (54%)
  Pallas kernels  3.35 us (27%)
  between operations  1.37 us (11%)
  local copies, waits for them, and re-layouts  0.84 us (7%)
    ppermute x3, starting transfers between devices, swapped(): lax.ppermute(shard, axis, [(i, partner(i) % size) for i in range(size)])  5.57 us
    pallas_call x1, Pallas kernels, on_device(): pl.pallas_call(functools.partial(late, geo), out_shape=jax.ShapeDtypeStru...  1.8 us
    ppermute x1, starting transfers between devices, across(): return lax.ppermute(shard, ('tm', 'diag'), pairs)  1.18 us
    pallas_call x1, Pallas kernels, on_device(): pl.pallas_call(functools.partial(early, geo), out_shape=jax.ShapeDtypeStr...  1.03 us
    unnamed x4, local copies, waits for them, and re-layouts  0.84 us
    pallas_call x1, Pallas kernels, on_device(): pl.pallas_call(functools.partial(prepare, geo), out_shape=[table] * 7, in...  0.48 us
  transfers between devices with their start and end apart: 4, of which 0 were waited for; matrix products, arithmetic and copies ran while one was open for 0% of the time, Pallas kernels for 13%

profile of v8, /device:TPU:1, one launch (start us, length us, event | category | flops | bytes accessed | tf_op | source)
XLA Modules:
  0.0 12.3 jit_solution(4595324826564483575)
XLA Ops:
  0.7 2.2 %collective-permute-start = (s32[128]{0:T(128)S(1)}, s32[128]{0:T(128)S(1)}, u32[]{:S(2)}, u32[]{:S(2)}) collective-permute-start(s32[128]{0:T(128)S(1)} %compare_select_fusion.1), channel_id=1, source_target_pairs={{0,1},{1,0},{2,3},{3,2},{4,5},{5,4},{6,7},{7,6},{8,9},{9,8},{10,11... | collective-permute-start | bytes 1544 | tf_op jit(solution)/shard_map/ppermute | solution.py:31
  2.8 0.0 copy-start
  2.8 0.8 %copy-done = f32[16384]{0:T(1024)S(1)} copy-done((f32[16384]{0:T(1024)S(1)}, f32[16384]{0:T(1024)}, u32[]{:S(2)}) %copy-start) | copy-done | bytes 65560
  3.7 1.0 %collective-permute-start.2 = (f32[96,128]{1,0:T(8,128)S(1)}, f32[96,128]{1,0:T(8,128)S(1)}, u32[]{:S(2)}, u32[]{:S(2)}) collective-permute-start(f32[96,128]{1,0:T(8,128)S(1)} %get-tuple-element.15), channel_id=1, source_target_pairs={{0,4},{4,0},{8,12},{12,8},{16,20},{20,16},{24,28},{28,24},{1,5},{5... | collective-permute-start | bytes 147464 | tf_op jit(solution)/shard_map/ppermute | solution.py:31
  4.7 0.0 copy-start.1
  4.7 1.2 %collective-permute-start.3 = (f32[96,128]{1,0:T(8,128)S(1)}, f32[96,128]{1,0:T(8,128)S(1)}, u32[]{:S(2)}, u32[]{:S(2)}) collective-permute-start(f32[96,128]{1,0:T(8,128)S(1)} %get-tuple-element.17), channel_id=1, source_target_pairs={{0,1},{1,0},{2,3},{3,2},{4,8},{5,9},{6,10},{7,11},{8,4},{9,5},{10,... | collective-permute-start | bytes 147464 | tf_op jit(solution)/shard_map/ppermute | solution.py:46
  6.6 0.0 collective-permute-done
  6.6 2.4 %collective-permute-start.1 = (s32[128]{0:T(128)S(1)}, s32[128]{0:T(128)S(1)}, u32[]{:S(2)}, u32[]{:S(2)}) collective-permute-start(s32[128]{0:T(128)S(1)} %get-tuple-element.26), channel_id=1, source_target_pairs={{0,2},{1,3},{2,0},{3,1},{4,6},{5,7},{6,4},{7,5},{8,10},{9,11},{10,... | collective-permute-start | bytes 1544 | tf_op jit(solution)/shard_map/ppermute | solution.py:31
  9.0 0.0 collective-permute-done.2.near_ref
  9.0 0.0 collective-permute-done.3.far_ref
  9.0 0.0 copy-done.1
  9.0 0.5 %prepare.1 = (f32[256,128]{1,0:T(8,128)S(1)}, f32[256,128]{1,0:T(8,128)S(1)}, f32[256,128]{1,0:T(8,128)S(1)}, f32[256,128]{1,0:T(8,128)S(1)}, f32[256,128]{1,0:T...) custom-call(f32[96,128]{1,0:T(8,128)S(1)} %collective-permute-done.2.near_ref, ...), custom_call_target="tpu_custom_call" | custom-call | flops 8388608 | bytes 1048576 | tf_op jit(solution)/shard_map/prepare/pallas_call | solution.py:334
  9.5 1.0 %early.1.before = f32[2080,128]{1,0:T(8,128)S(1)} custom-call(s32[1,128]{1,0:T(1,128)S(1)} %get-tuple-element.25.mine_ref, f32[256,128]{1,0:T(8,128)S(1)} %get-tuple-element.18.refs_0_, f32[256,128]{1,0:T(8,128)S(1)} %get-tuple-element.19.refs_1_, f32[256,128]{1,0:T(8,128)S(1)} %get-tuple-element.20.refs_2_, f32[256,128]{1,0:T(8,128)S(1)} %get-tuple-element.21.refs_3_, ...), custom_call_target="tpu_custom_call" | custom-call | flops 8388608 | bytes 1048576 | tf_op jit(solution)/shard_map/early/pallas_call | solution.py:351
  10.5 0.0 collective-permute-done.1
  10.5 1.8 %late.1 = f32[32,128]{1,0:T(8,128)} custom-call(s32[1,128]{1,0:T(1,128)S(1)} %get-tuple-element.25.mine_ref, s32[1,128]{1,0:T(1,128)S(1)} %bitcast.13, f32[2080,128]{1,0:T(8,128)S(1)} %early.1.before, f32[256,128]{1,0:T(8,128)S(1)} %get-tuple-element.18.refs_0_, f32[256,128]{1,0:T(8,128)S(1)} %get-tuple-element.19.refs_1_, ...), custom_call_target="tpu_custom_call" | custom-call | flops 16777216 | bytes 1048576 | tf_op jit(solution)/shard_map/late/pallas_call | solution.py:361
  (4 shorter events, 0.0 us)
Async XLA Ops:
  0.7 5.9 %collective-permute-start = (s32[128]{0:T(128)S(1)}, s32[128]{0:T(128)S(1)}, u32[]{:S(2)}, u32[]{:S(2)}) collective-permute-start(s32[128]{0:T(128)S(1)} %compare_select_fusion.1), channel_id=1, source_target_pairs={{0,1},{1,0},{2,3},{3,2},{4,5},{5,4},{6,7},{7,6},{8,9},{9,8},{10,11... | collective-permute-start | bytes 1544 | tf_op jit(solution)/shard_map/ppermute | solution.py:31
  2.8 0.8 %copy-start = (f32[16384]{0:T(1024)S(1)}, f32[16384]{0:T(1024)}, u32[]{:S(2)}) copy-start(f32[16384]{0:T(1024)} %param.4) | copy-start | bytes 196612
  3.7 5.3 %collective-permute-start.2 = (f32[96,128]{1,0:T(8,128)S(1)}, f32[96,128]{1,0:T(8,128)S(1)}, u32[]{:S(2)}, u32[]{:S(2)}) collective-permute-start(f32[96,128]{1,0:T(8,128)S(1)} %get-tuple-element.15), channel_id=1, source_target_pairs={{0,4},{4,0},{8,12},{12,8},{16,20},{20,16},{24,28},{28,24},{1,5},{5... | collective-permute-start | bytes 147464 | tf_op jit(solution)/shard_map/ppermute | solution.py:31
  4.7 4.3 %copy-start.1 = (f32[256]{0:T(256)S(1)}, f32[256]{0:T(256)}, u32[]{:S(2)}) copy-start(f32[256]{0:T(256)} %param.5) | copy-start | bytes 3076
  4.7 4.3 %collective-permute-start.3 = (f32[96,128]{1,0:T(8,128)S(1)}, f32[96,128]{1,0:T(8,128)S(1)}, u32[]{:S(2)}, u32[]{:S(2)}) collective-permute-start(f32[96,128]{1,0:T(8,128)S(1)} %get-tuple-element.17), channel_id=1, source_target_pairs={{0,1},{1,0},{2,3},{3,2},{4,8},{5,9},{6,10},{7,11},{8,4},{9,5},{10,... | collective-permute-start | bytes 147464 | tf_op jit(solution)/shard_map/ppermute | solution.py:46
  6.6 3.9 %collective-permute-start.1 = (s32[128]{0:T(128)S(1)}, s32[128]{0:T(128)S(1)}, u32[]{:S(2)}, u32[]{:S(2)}) collective-permute-start(s32[128]{0:T(128)S(1)} %get-tuple-element.26), channel_id=1, source_target_pairs={{0,2},{1,3},{2,0},{3,1},{4,6},{5,7},{6,4},{7,5},{8,10},{9,11},{10,... | collective-permute-start | bytes 1544 | tf_op jit(solution)/shard_map/ppermute | solution.py:31
